TPU v7x, 128 devices: a whole 4x4x4 slice. The times are simulated.
128 devices in a mesh: data: 1, dap: 128 (over z, y, x, core).
Axes of the slice: x: 4, y: 4, z: 4, core: 2. Of those that a mesh axis runs over, the one named last changes fastest.
Arguments:
- z: bfloat16 [1024, 1024, 64], P(('data', 'dap'))
- res_mask: int32 [1024], P('data')
- ln_w: bfloat16 [3, 2, 2, 64], replicated
- w_in: bfloat16 [3, 2, 64, 256], replicated
- b_g: bfloat16 [3, 2, 64], replicated
- w_b: bfloat16 [3, 2, 64, 4], replicated
- w_o: bfloat16 [3, 2, 64, 64], replicated
- b_o: bfloat16 [3, 2, 64], replicated
Outputs:
- output: bfloat16 [1024, 1024, 64], P(('data', 'dap'))
All inputs are finite; a program needn't handle non-finite values.
Results may differ from a plain program's by a relative error of at most 0.0117227.
Values are sent between devices in bfloat16 or wider.
A program may use at most 1 GiB of HBM per device.

v0:
```python
import math
import jax
import jax.numpy as jnp
from jax import lax
from jax.sharding import PartitionSpec as P

EPS = 1e-5
NEG = -1e9
F32 = jnp.float32
BF16 = jnp.bfloat16


def _ln(x, w):
    x = x.astype(F32)
    mu = jnp.mean(x, axis=-1, keepdims=True)
    var = jnp.mean(jnp.square(x - mu), axis=-1, keepdims=True)
    y = (x - mu) * lax.rsqrt(var + EPS)
    return (y * w[0].astype(F32) + w[1].astype(F32)).astype(BF16)


def _rows(zl, bias, lw, wi, bg, wo, bo):
    r, n, c = zl.shape
    h = bias.shape[0]
    d = wo.shape[0] // h
    rb = math.gcd(r, 8)
    gate_b = bg.astype(F32).reshape(h, d)

    def block(zb):
        y = _ln(zb, lw)
        proj = jnp.dot(y.reshape(rb * n, c), wi, preferred_element_type=F32).reshape(rb, n, 4, h, d)
        q = proj[:, :, 0].astype(BF16)
        k = proj[:, :, 1].astype(BF16)
        v = proj[:, :, 2].astype(BF16)
        gate = jax.nn.sigmoid(proj[:, :, 3] + gate_b)
        s = jnp.einsum('bjhd,bkhd->bhjk', q, k, preferred_element_type=F32) * d ** -0.5 + bias
        p = jax.nn.softmax(s, axis=-1).astype(BF16)
        o = jnp.einsum('bhjk,bkhd->bjhd', p, v, preferred_element_type=F32)
        o = (gate * o).astype(BF16).reshape(rb * n, h * d)
        upd = jnp.dot(o, wo, preferred_element_type=F32) + bo.astype(F32)
        return (zb.astype(F32) + upd.reshape(rb, n, c)).astype(BF16)

    out = lax.map(block, zl.reshape(r // rb, rb, n, c))
    return out.reshape(r, n, c)


def _tri_start(zl, mask_bias, lw, wi, bg, wb, wo, bo):
    r, n, c = zl.shape
    b = jnp.dot(_ln(zl, lw).reshape(r * n, c), wb, preferred_element_type=F32).astype(BF16)
    b = lax.all_gather(b.reshape(r, n, -1), 'dap', axis=0, tiled=True)
    bias = jnp.transpose(b, (2, 0, 1)).astype(F32) + mask_bias
    return _rows(zl, bias, lw, wi, bg, wo, bo)


def solution(mesh):
    def local(zl, res_mask, ln_w, w_in, b_g, w_b, w_o, b_o):
        mask_bias = jnp.where(res_mask > 0, 0.0, NEG).astype(F32)
        ws = (ln_w, w_in, b_g, w_b, w_o, b_o)
        for l in range(ln_w.shape[0]):
            zl = _tri_start(zl, mask_bias, *(a[l, 0] for a in ws))
            zt = lax.all_to_all(zl, 'dap', 1, 0, tiled=True)
            zt = _tri_start(jnp.swapaxes(zt, 0, 1), mask_bias, *(a[l, 1] for a in ws))
            zl = lax.all_to_all(jnp.swapaxes(zt, 0, 1), 'dap', 0, 1, tiled=True)
        return zl

    rows = P(('data', 'dap'))
    return jax.shard_map(local, mesh=mesh,
                         in_specs=(rows, P('data'), P(), P(), P(), P(), P(), P()),
                         out_specs=rows, check_vma=False)
```

profile of v0, /device:TPU:1, one launch (start us, length us, event | category | flops | bytes accessed | tf_op | source)
XLA Modules:
  0.0 1533.4 jit_solution(12570036147283844415)
XLA Ops:
  22.9 64.9 %all-gather.7.cloned.1.call-done = bf16[1024,1024,4]{1,2,0:T(4,128)(2,1)} async-done(((bf16[8,1024,4]{1,2,0:T(4,128)(2,1)}), bf16[1024,1024,4]{1,2,0:T(4,128)(2,1)}) %all-gather.7.cloned.1.call-update) | async-done | bytes 8388624 | tf_op jit(solution)/shard_map/all_gather | solution.py:49
  97.7 19.2 %copy.348 = f32[4,1024,1024]{1,2,0:T(8,128)} copy(f32[4,1024,1024]{2,0,1:T(4,128)} %add_bitcast_fusion.5) | data formatting | bytes 33554432 | tf_op jit(solution)/shard_map/add | solution.py:50
  116.9 56.9 %fusion.151 = (f32[8,4,1024]{2,1,0:T(4,128)S(1)}, f32[8,4,1024,1024]{2,3,1,0:T(8,128)}) fusion(f32[4,1024,1024]{1,2,0:T(8,128)} %copy.348, bf16[8,1024,4,4,16]{1,4,3,2,0:T(8,128)(2,1)} %get-tuple-element.168), kind=kOutput, calls=%fused_computation.270 | convolution fusion | flops 1207960576 | bytes 153223168 | tf_op jit(solution)/shard_map/while/body/eval_jaxpr/sub | solution.py:36
  173.8 42.3 %fusion.102 = bf16[8,1024,4,16]{1,3,2,0:T(8,128)(2,1)S(1)} fusion(f32[8,1024,4,4,16]{1,4,3,2,0:T(8,128)} %get-tuple-element.169, f32[8,4,1024,1024]{2,3,1,0:T(8,128)} %get-tuple-element.180, f32[8,4,1024]{2,1,0:T(4,128)S(1)} %get-tuple-element.170, bf16[8,1024,4,4,16]{1,4,3,2,0:T(8,128)(2,1)} %get-tuple-element.168, f32[4,16]{1,0:T(4,128)S(1)} %reshape.803), kind=kOutput, calls=%fused_computation.161 | convolution fusion | flops 1143996416 | bytes 138543360 | tf_op jit(solution)/shard_map/while/body/eval_jaxpr/bhjk,bkhd->bjhd/dot_general | solution.py:37
  222.2 24.7 %all_to_all.63 = bf16[128,2,2048]{2,1,0:T(2,128)(2,1)} all-to-all(bf16[128,2,2048]{2,1,0:T(2,128)(2,1)S(1)} %reshape.881), channel_id=1, replica_groups=mesh['data'=1,'dap'=128] {'dap'}, dimensions={0} | all-to-all | bytes 2097152 | tf_op jit(solution)/shard_map/all_to_all | solution.py:60
  284.4 60.1 %all-gather.9.cloned.1.call-done = bf16[1024,1024,4]{1,2,0:T(4,128)(2,1)} async-done(((bf16[8,1024,4]{1,2,0:T(4,128)(2,1)}), bf16[1024,1024,4]{1,2,0:T(4,128)(2,1)}) %all-gather.9.cloned.1.call-update) | async-done | bytes 8388624 | tf_op jit(solution)/shard_map/all_gather | solution.py:49
  344.5 10.4 add_bitcast_fusion.4
  354.9 19.2 %copy.365 = f32[4,1024,1024]{1,2,0:T(8,128)} copy(f32[4,1024,1024]{2,0,1:T(4,128)} %add_bitcast_fusion.4) | data formatting | bytes 33554432 | tf_op jit(solution)/shard_map/add | solution.py:50
  374.1 56.9 %fusion.153 = (f32[8,4,1024]{2,1,0:T(4,128)S(1)}, f32[8,4,1024,1024]{2,3,1,0:T(8,128)}) fusion(f32[4,1024,1024]{1,2,0:T(8,128)} %copy.365, bf16[8,1024,4,4,16]{1,4,3,2,0:T(8,128)(2,1)} %get-tuple-element.181), kind=kOutput, calls=%fused_computation.272 | convolution fusion | flops 1207960576 | bytes 153223168 | tf_op jit(solution)/shard_map/while/body/eval_jaxpr/sub | solution.py:36
  431.1 42.4 %fusion.103 = bf16[8,1024,4,16]{1,3,2,0:T(8,128)(2,1)S(1)} fusion(f32[8,1024,4,4,16]{1,4,3,2,0:T(8,128)} %get-tuple-element.182, f32[8,4,1024,1024]{2,3,1,0:T(8,128)} %get-tuple-element.184, f32[8,4,1024]{2,1,0:T(4,128)S(1)} %get-tuple-element.183, bf16[8,1024,4,4,16]{1,4,3,2,0:T(8,128)(2,1)} %get-tuple-element.181, f32[4,16]{1,0:T(4,128)S(1)} %reshape.807), kind=kOutput, calls=%fused_computation.162 | convolution fusion | flops 1143996416 | bytes 138543360 | tf_op jit(solution)/shard_map/while/body/eval_jaxpr/bhjk,bkhd->bjhd/dot_general | solution.py:37
  486.0 24.7 %all_to_all.64 = bf16[128,2,2048]{2,1,0:T(2,128)(2,1)} all-to-all(bf16[128,2,2048]{2,1,0:T(2,128)(2,1)S(1)} %reshape.883), channel_id=1, replica_groups=mesh['data'=1,'dap'=128] {'dap'}, dimensions={0} | all-to-all | bytes 2097152 | tf_op jit(solution)/shard_map/all_to_all | solution.py:62
  537.3 53.9 %all-gather.11.cloned.1.call-done = bf16[1024,1024,4]{1,2,0:T(4,128)(2,1)} async-done(((bf16[8,1024,4]{1,2,0:T(4,128)(2,1)}), bf16[1024,1024,4]{1,2,0:T(4,128)(2,1)}) %all-gather.11.cloned.1.call-update) | async-done | bytes 8388624 | tf_op jit(solution)/shard_map/all_gather | solution.py:49
  601.2 19.2 %copy.376 = f32[4,1024,1024]{1,2,0:T(8,128)} copy(f32[4,1024,1024]{2,0,1:T(4,128)} %add_bitcast_fusion.3) | data formatting | bytes 33554432 | tf_op jit(solution)/shard_map/add | solution.py:50
  620.4 56.9 %fusion.155 = (f32[8,4,1024]{2,1,0:T(4,128)S(1)}, f32[8,4,1024,1024]{2,3,1,0:T(8,128)}) fusion(f32[4,1024,1024]{1,2,0:T(8,128)} %copy.376, bf16[8,1024,4,4,16]{1,4,3,2,0:T(8,128)(2,1)} %get-tuple-element.185), kind=kOutput, calls=%fused_computation.274 | convolution fusion | flops 1207960576 | bytes 153223168 | tf_op jit(solution)/shard_map/while/body/eval_jaxpr/sub | solution.py:36
  677.3 42.3 %fusion.104 = bf16[8,1024,4,16]{1,3,2,0:T(8,128)(2,1)S(1)} fusion(f32[8,1024,4,4,16]{1,4,3,2,0:T(8,128)} %get-tuple-element.186, f32[8,4,1024,1024]{2,3,1,0:T(8,128)} %get-tuple-element.188, f32[8,4,1024]{2,1,0:T(4,128)S(1)} %get-tuple-element.187, bf16[8,1024,4,4,16]{1,4,3,2,0:T(8,128)(2,1)} %get-tuple-element.185, f32[4,16]{1,0:T(4,128)S(1)} %reshape.812), kind=kOutput, calls=%fused_computation.163 | convolution fusion | flops 1143996416 | bytes 138543360 | tf_op jit(solution)/shard_map/while/body/eval_jaxpr/bhjk,bkhd->bjhd/dot_general | solution.py:37
  726.2 24.7 %all_to_all.65 = bf16[128,2,2048]{2,1,0:T(2,128)(2,1)} all-to-all(bf16[128,2,2048]{2,1,0:T(2,128)(2,1)S(1)} %reshape.885), channel_id=1, replica_groups=mesh['data'=1,'dap'=128] {'dap'}, dimensions={0} | all-to-all | bytes 2097152 | tf_op jit(solution)/shard_map/all_to_all | solution.py:60
  788.4 60.1 %all-gather.13.cloned.1.call-done = bf16[1024,1024,4]{1,2,0:T(4,128)(2,1)} async-done(((bf16[8,1024,4]{1,2,0:T(4,128)(2,1)}), bf16[1024,1024,4]{1,2,0:T(4,128)(2,1)}) %all-gather.13.cloned.1.call-update) | async-done | bytes 8388624 | tf_op jit(solution)/shard_map/all_gather | solution.py:49
  848.6 10.1 add_bitcast_fusion.2
  858.7 19.2 %copy.394 = f32[4,1024,1024]{1,2,0:T(8,128)} copy(f32[4,1024,1024]{2,0,1:T(4,128)} %add_bitcast_fusion.2) | data formatting | bytes 33554432 | tf_op jit(solution)/shard_map/add | solution.py:50
  877.9 56.9 %fusion.157 = (f32[8,4,1024]{2,1,0:T(4,128)S(1)}, f32[8,4,1024,1024]{2,3,1,0:T(8,128)}) fusion(f32[4,1024,1024]{1,2,0:T(8,128)} %copy.394, bf16[8,1024,4,4,16]{1,4,3,2,0:T(8,128)(2,1)} %get-tuple-element.198), kind=kOutput, calls=%fused_computation.276 | convolution fusion | flops 1207960576 | bytes 153223168 | tf_op jit(solution)/shard_map/while/body/eval_jaxpr/sub | solution.py:36
  934.8 42.4 %fusion.105 = bf16[8,1024,4,16]{1,3,2,0:T(8,128)(2,1)S(1)} fusion(f32[8,1024,4,4,16]{1,4,3,2,0:T(8,128)} %get-tuple-element.199, f32[8,4,1024,1024]{2,3,1,0:T(8,128)} %get-tuple-element.201, f32[8,4,1024]{2,1,0:T(4,128)S(1)} %get-tuple-element.200, bf16[8,1024,4,4,16]{1,4,3,2,0:T(8,128)(2,1)} %get-tuple-element.198, f32[4,16]{1,0:T(4,128)S(1)} %reshape.816), kind=kOutput, calls=%fused_computation.164 | convolution fusion | flops 1143996416 | bytes 138543360 | tf_op jit(solution)/shard_map/while/body/eval_jaxpr/bhjk,bkhd->bjhd/dot_general | solution.py:37
  989.9 24.7 %all_to_all.66 = bf16[128,2,2048]{2,1,0:T(2,128)(2,1)} all-to-all(bf16[128,2,2048]{2,1,0:T(2,128)(2,1)S(1)} %reshape.887), channel_id=1, replica_groups=mesh['data'=1,'dap'=128] {'dap'}, dimensions={0} | all-to-all | bytes 2097152 | tf_op jit(solution)/shard_map/all_to_all | solution.py:62
  1041.3 53.9 %all-gather.15.cloned.1.call-done = bf16[1024,1024,4]{1,2,0:T(4,128)(2,1)} async-done(((bf16[8,1024,4]{1,2,0:T(4,128)(2,1)}), bf16[1024,1024,4]{1,2,0:T(4,128)(2,1)}) %all-gather.15.cloned.1.call-update) | async-done | bytes 8388624 | tf_op jit(solution)/shard_map/all_gather | solution.py:49
  1105.2 19.2 %copy.405 = f32[4,1024,1024]{1,2,0:T(8,128)} copy(f32[4,1024,1024]{2,0,1:T(4,128)} %add_bitcast_fusion.1) | data formatting | bytes 33554432 | tf_op jit(solution)/shard_map/add | solution.py:50
  1124.4 56.9 %fusion.159 = (f32[8,4,1024]{2,1,0:T(4,128)S(1)}, f32[8,4,1024,1024]{2,3,1,0:T(8,128)}) fusion(f32[4,1024,1024]{1,2,0:T(8,128)} %copy.405, bf16[8,1024,4,4,16]{1,4,3,2,0:T(8,128)(2,1)} %get-tuple-element.202), kind=kOutput, calls=%fused_computation.278 | convolution fusion | flops 1207960576 | bytes 153223168 | tf_op jit(solution)/shard_map/while/body/eval_jaxpr/sub | solution.py:36
  1181.3 42.3 %fusion.106 = bf16[8,1024,4,16]{1,3,2,0:T(8,128)(2,1)S(1)} fusion(f32[8,1024,4,4,16]{1,4,3,2,0:T(8,128)} %get-tuple-element.203, f32[8,4,1024,1024]{2,3,1,0:T(8,128)} %get-tuple-element.205, f32[8,4,1024]{2,1,0:T(4,128)S(1)} %get-tuple-element.204, bf16[8,1024,4,4,16]{1,4,3,2,0:T(8,128)(2,1)} %get-tuple-element.202, f32[4,16]{1,0:T(4,128)S(1)} %reshape.821), kind=kOutput, calls=%fused_computation.165 | convolution fusion | flops 1143996416 | bytes 138543360 | tf_op jit(solution)/shard_map/while/body/eval_jaxpr/bhjk,bkhd->bjhd/dot_general | solution.py:37
  1230.0 24.7 %all_to_all.67 = bf16[128,2,2048]{2,1,0:T(2,128)(2,1)} all-to-all(bf16[128,2,2048]{2,1,0:T(2,128)(2,1)S(1)} %reshape.889), channel_id=1, replica_groups=mesh['data'=1,'dap'=128] {'dap'}, dimensions={0} | all-to-all | bytes 2097152 | tf_op jit(solution)/shard_map/all_to_all | solution.py:60
  1292.1 60.2 %all-gather.17.cloned.1.call-done = bf16[1024,1024,4]{1,2,0:T(4,128)(2,1)} async-done(((bf16[8,1024,4]{1,2,0:T(4,128)(2,1)}), bf16[1024,1024,4]{1,2,0:T(4,128)(2,1)}) %all-gather.17.cloned.1.call-update) | async-done | bytes 8388624 | tf_op jit(solution)/shard_map/all_gather | solution.py:49
  1362.3 19.2 %copy.423 = f32[4,1024,1024]{1,2,0:T(8,128)} copy(f32[4,1024,1024]{2,0,1:T(4,128)} %add_bitcast_fusion) | data formatting | bytes 33554432 | tf_op jit(solution)/shard_map/add | solution.py:50
  1381.5 57.2 %fusion.161 = (f32[8,4,1024]{2,1,0:T(4,128)S(1)}, f32[8,4,1024,1024]{2,3,1,0:T(8,128)}) fusion(f32[4,1024,1024]{1,2,0:T(8,128)} %copy.423, bf16[8,1024,4,4,16]{1,4,3,2,0:T(8,128)(2,1)} %get-tuple-element.206), kind=kOutput, calls=%fused_computation.280 | convolution fusion | flops 1207960576 | bytes 153223168 | tf_op jit(solution)/shard_map/while/body/eval_jaxpr/sub | solution.py:36
  1438.6 42.4 %fusion.107 = bf16[8,1024,4,16]{1,3,2,0:T(8,128)(2,1)S(1)} fusion(f32[8,1024,4,4,16]{1,4,3,2,0:T(8,128)} %get-tuple-element.216, f32[8,4,1024,1024]{2,3,1,0:T(8,128)} %get-tuple-element.220, f32[8,4,1024]{2,1,0:T(4,128)S(1)} %get-tuple-element.218, bf16[8,1024,4,4,16]{1,4,3,2,0:T(8,128)(2,1)} %get-tuple-element.206, f32[4,16]{1,0:T(4,128)S(1)} %reshape.825), kind=kOutput, calls=%fused_computation.166 | convolution fusion | flops 1143996416 | bytes 138543360 | tf_op jit(solution)/shard_map/while/body/eval_jaxpr/bhjk,bkhd->bjhd/dot_general | solution.py:37
  1493.3 24.7 %all_to_all.68 = bf16[128,2,2048]{2,1,0:T(2,128)(2,1)} all-to-all(bf16[128,2,2048]{2,1,0:T(2,128)(2,1)S(1)} %reshape.891), channel_id=1, replica_groups=mesh['data'=1,'dap'=128] {'dap'}, dimensions={0} | all-to-all | bytes 2097152 | tf_op jit(solution)/shard_map/all_to_all | solution.py:62
  (244 shorter events, 285.4 us)
Async XLA Ops:
  6.5 10.0 copy-start
  6.5 7.9 copy-start.14
  6.5 8.7 copy-start.20
  6.5 9.4 copy-start.21
  6.5 10.0 copy-start.22
  6.5 81.2 %all-gather.7.cloned.1.call-start = ((), (), s32[]{:S(2)}) async-start(), calls=%async_computation.6 | async-start | bytes 8454144 | tf_op jit(solution)/shard_map/all_gather | solution.py:49
  14.4 330.1 %all-gather.9.cloned.1.call-start = ((), (), s32[]{:S(2)}) async-start(), calls=%async_computation.7 | async-start | bytes 8454144 | tf_op jit(solution)/shard_map/all_gather | solution.py:49
  16.6 71.2 %copy-start.8 = (f32[1024]{0:T(1024)}, f32[1024]{0:T(1024)S(1)}, u32[]{:S(2)}) copy-start(f32[1024]{0:T(1024)S(1)} %compare_select_fusion) | copy-start | bytes 12292
  262.6 5.3 copy-start.31
  262.6 5.3 copy-start.32
  273.6 4.8 copy-start.19
  273.6 4.9 copy-start.37
  278.4 312.8 %all-gather.11.cloned.1.call-start = ((), (), s32[]{:S(2)}) async-start(), calls=%async_computation.8 | async-start | bytes 8454144 | tf_op jit(solution)/shard_map/all_gather | solution.py:49
  278.7 65.9 %copy-start.9 = (f32[1024]{0:T(1024)S(1)}, f32[1024]{0:T(1024)}, u32[]{:S(2)}) copy-start(f32[1024]{0:T(1024)} %copy-done.8) | copy-start | bytes 12292
  514.4 4.0 copy-start.29
  514.4 4.0 copy-start.30
  525.1 323.5 %all-gather.13.cloned.1.call-start = ((), (), s32[]{:S(2)}) async-start(), calls=%async_computation.9 | async-start | bytes 8454144 | tf_op jit(solution)/shard_map/all_gather | solution.py:49
  531.5 59.7 %copy-start.10 = (f32[1024]{0:T(1024)S(1)}, f32[1024]{0:T(1024)}, u32[]{:S(2)}) copy-start(f32[1024]{0:T(1024)} %copy-done.8) | copy-start | bytes 12292
  766.6 5.3 copy-start.27
  766.6 5.3 copy-start.28
  777.7 4.8 copy-start.17
  777.7 4.9 copy-start.35
  782.4 312.8 %all-gather.15.cloned.1.call-start = ((), (), s32[]{:S(2)}) async-start(), calls=%async_computation.10 | async-start | bytes 8454144 | tf_op jit(solution)/shard_map/all_gather | solution.py:49
  782.7 65.9 %copy-start.11 = (f32[1024]{0:T(1024)S(1)}, f32[1024]{0:T(1024)}, u32[]{:S(2)}) copy-start(f32[1024]{0:T(1024)} %copy-done.8) | copy-start | bytes 12292
  1018.4 4.0 copy-start.25
  1029.1 323.2 %all-gather.17.cloned.1.call-start = ((), (), s32[]{:S(2)}) async-start(), calls=%async_computation.11 | async-start | bytes 8454144 | tf_op jit(solution)/shard_map/all_gather | solution.py:49
  1035.5 59.7 %copy-start.12 = (f32[1024]{0:T(1024)S(1)}, f32[1024]{0:T(1024)}, u32[]{:S(2)}) copy-start(f32[1024]{0:T(1024)} %copy-done.8) | copy-start | bytes 12292
  1270.4 5.3 copy-start.23
  1270.4 5.3 copy-start.24
  1281.4 4.8 copy-start.15
  1281.4 4.9 copy-start.33
  1286.4 65.9 %copy-start.13 = (f32[1024]{0:T(1024)S(1)}, f32[1024]{0:T(1024)}, u32[]{:S(2)}) copy-start(f32[1024]{0:T(1024)} %copy-done.8) | copy-start | bytes 12292
  (18 other events, 39.1 us)
Sparse Core Ops, SparseCore 0:
  14.5 73.1 all-gather.6
  278.5 65.9 all-gather.8
  525.2 65.9 all-gather.10
  782.5 65.9 all-gather.12
  1029.2 65.9 all-gather.14
  1286.3 65.9 all-gather.16
where the time goes:
time: 1550 us; the launch traced here: 1530 us
  matrix products  649 us (42%)
  waiting for transfers between devices  353 us (23%)
  local copies, waits for them, and re-layouts  229 us (15%)
  blocking collectives  148 us (10%)
  other arithmetic  140 us (9%)
    all_gather x6, waiting for transfers between devices, _tri_start(): b = lax.all_gather(b.reshape(r, n, -1), 'dap', axis=0, tiled=True)  353 us
    sub x6, matrix products, block(): p = jax.nn.softmax(s, axis=-1).astype(BF16)  342 us
    dot_general x6, matrix products, block(): o = jnp.einsum('bhjk,bkhd->bjhd', p, v, preferred_element_type=F32)  254 us
    add x6, local copies, waits for them, and re-layouts, _tri_start(): bias = jnp.transpose(b, (2, 0, 1)).astype(F32) + mask_bias  115 us
    all_to_all x3, blocking collectives, local(): zt = lax.all_to_all(zl, 'dap', 1, 0, tiled=True)  74 us
    all_to_all x3, blocking collectives, local(): zl = lax.all_to_all(jnp.swapaxes(zt, 0, 1), 'dap', 0, 1, tiled=True)  74 us
    add x6, other arithmetic, _tri_start(): bias = jnp.transpose(b, (2, 0, 1)).astype(F32) + mask_bias  60.4 us
    unnamed x112, local copies, waits for them, and re-layouts  44.6 us
  transfers between devices with their start and end apart: 6, of which 6 were waited for; matrix products, arithmetic and copies ran while one was open for 3% of the time, Pallas kernels for 0%

commit v1 on v0

v1 whole, which is shorter than its diff:
```python
import functools, math
import jax, jax.numpy as jnp
from jax import lax
from jax.experimental import pallas as pl
from jax.experimental.pallas import tpu as pltpu
from jax.sharding import PartitionSpec as P
F32=jnp.float32; BF16=jnp.bfloat16
EPS=1e-5; NEG=-1e9
LOG2E=1.4426950408889634
MX=256

def _ln_t(x, gamma, beta):
    mu = jnp.mean(x, axis=0, keepdims=True)
    d = x - mu
    var = jnp.mean(d*d, axis=0, keepdims=True)
    return (d * lax.rsqrt(var + EPS) * gamma + beta).astype(BF16)

def fast_kernel(R, N, C, H, LAG, NR, OA, FD,
               z_ref, bias_ref, mask_ref, lnw_ref, wqvt_ref, wk2_ref, bg_ref, wo_ref, bo_ref, lnn_ref, wbn_ref,
               out_ref, bnext_ref,
               k_s, q_s, v_s, g_s, o_s, y_s, bias_s):
    jb = pl.program_id(0)
    D = C // H
    QB = MX
    KC = 128
    CH = N // KC
    q0 = pl.multiple_of(jb * QB, QB)

    def body(*accs):
        sacc = [accs[0:NR], accs[NR:2*NR]]
        oacc = [accs[2*NR:2*NR+OA], accs[2*NR+OA:2*NR+2*OA]]
        z128 = jnp.zeros((KC, MX-KC), BF16)
        zrow = lambda n: jnp.zeros((n, MX), BF16)

        @pl.when(jb == 0)
        def _():
            def prep(i, _):
                y = _ln_t(z_ref[i].astype(F32), lnw_ref[:, 0:1], lnw_ref[:, 1:2])
                yt = jnp.concatenate([y, jnp.zeros((KC-C, N), BF16)], axis=0).T
                for j in range(N//MX):
                    m = j % 2
                    cs = slice(j*MX, (j+1)*MX)
                    pltpu.matmul_push_rhs(jnp.concatenate([y[:, cs], zrow(MX-C)], axis=0), staging_register=0, mxu_index=m)
                    pltpu.matmul_acc_lhs(sacc[m][0], wqvt_ref[0:KC], load_staged_rhs=0)
                    pltpu.matmul_acc_lhs(sacc[m][1], wqvt_ref[KC:2*KC])
                    pltpu.matmul_push_rhs(wk2_ref[...], staging_register=1, mxu_index=m)
                    for r in range(2):
                        kk = jnp.concatenate([yt[j*MX+r*KC:j*MX+(r+1)*KC], z128], axis=1)
                        pltpu.matmul_acc_lhs(sacc[m][2+r], kk, load_staged_rhs=1 if r == 0 else None)
                    qv = pltpu.matmul_pop(sacc[m][0])
                    q = qv[0:C].astype(BF16).astype(F32) * (LOG2E * D ** -0.5)
                    qh = q.astype(BF16)
                    ql = (q - qh.astype(F32)).astype(BF16)
                    for h in range(H):
                        q_s[i, 2*D*h:2*D*h+D, cs] = qh[D*h:D*h+D]
                        q_s[i, 2*D*h+D:2*D*h+2*D, cs] = ql[D*h:D*h+D]
                    v_s[i, :, cs] = qv[C:2*C].astype(BF16)
                    t = pltpu.matmul_pop(sacc[m][1])
                    g_s[i, :, cs] = jax.nn.sigmoid(t[0:C] + bg_ref[...])
                    for r in range(2):
                        k_s[i, j*MX+r*KC:j*MX+(r+1)*KC] = pltpu.matmul_pop(sacc[m][2+r])[:, 0:2*C].astype(BF16)
                return 0
            lax.fori_loop(0, R, prep, 0)

        for h in range(H):
            for c in range(CH):
                sl = slice(c*KC, (c+1)*KC)
                for w in range(2):
                    bias_s[h, sl, w*128:(w+1)*128] = bias_ref[h, sl, w*128:(w+1)*128].astype(F32) * LOG2E + mask_ref[sl]

        zp = jnp.zeros((KC, QB), BF16)
        zv = jnp.zeros((2*D, MX-KC), BF16)
        zq = jnp.zeros((2*D, QB), BF16)
        ones = jnp.where(lax.broadcasted_iota(jnp.int32, (D, KC), 0) == 0, 1.0, 0.0).astype(BF16)
        steps = [(h, c) for h in range(H) for c in range(CH)]
        S = len(steps)

        def pair(t, _):
            es = {}
            def tile(n):
                for m in range(2):
                    p = es.pop((n, m)) if n >= 0 else zp
                    if n+LAG < S:
                        h, c = steps[n+LAG]
                        w = jnp.concatenate([zq]*h + [q_s[2*t+m, 2*D*h:2*D*(h+1), pl.ds(q0, QB)]] + [zq]*(H-1-h), axis=0)
                    else:
                        w = zp
                    pltpu.matmul_push_rhs(jnp.concatenate([p, w], axis=0), staging_register=n % 2, mxu_index=m)
            def accum(n):
                for m in range(2):
                    ld = n % 2
                    if n+LAG < S:
                        h, c = steps[n+LAG]
                        kk = jnp.concatenate([z128, k_s[2*t+m, c*KC:(c+1)*KC]], axis=1)
                        pltpu.matmul_acc_lhs(sacc[m][(n+LAG) % NR], kk, load_staged_rhs=ld)
                        ld = None
                    if n >= 0:
                        h, c = steps[n]
                        vv = jnp.concatenate([v_s[2*t+m, D*h:D*h+D, c*KC:(c+1)*KC], ones], axis=0)
                        pltpu.matmul_acc_lhs(oacc[m][h % OA], jnp.concatenate([vv, zv], axis=1), load_staged_rhs=ld)
            def ex(n):
                h, c = steps[n]
                b = bias_s[h, c*KC:(c+1)*KC]
                for m in range(2):
                    es[n, m] = jnp.exp2(pltpu.matmul_pop(sacc[m][n % NR]) + b).astype(BF16)
            def fin(n):
                h, c = steps[n]
                if c == CH-1:
                    for m in range(2):
                        i = 2*t+m
                        a = pltpu.matmul_pop(oacc[m][h % OA])
                        o_s[i, D*h:D*h+D] = (g_s[i, D*h:D*h+D, pl.ds(q0, QB)] * (a[0:D] / a[D:D+1])).astype(BF16)
            for n in range(-LAG, S):
                if n >= 0: ex(n)
                tile(n); accum(n)
                if n-FD >= 0: fin(n-FD)
            for n in range(S-FD, S): fin(n)
            return 0
        lax.fori_loop(0, R//2, pair, 0)

        def upd(t, _):
            for m in range(2):
                pltpu.matmul_push_rhs(jnp.concatenate([o_s[2*t+m], zrow(MX-C)], axis=0), staging_register=0, mxu_index=m)
                pltpu.matmul_acc_lhs(sacc[m][0], wo_ref[...], load_staged_rhs=0)
            for m in range(2):
                i = 2*t+m
                u = pltpu.matmul_pop(sacc[m][0])[0:C] + bo_ref[...]
                zn = (z_ref[i, :, pl.ds(q0, QB)].astype(F32) + u).astype(BF16)
                out_ref[i] = zn
                y_s[pl.ds(pl.multiple_of(i*C, C), C)] = _ln_t(zn.astype(F32), lnn_ref[:, 0:1], lnn_ref[:, 1:2])
            return 0
        lax.fori_loop(0, R//2, upd, 0)
        for m in range(2):
            pltpu.matmul_push_rhs(y_s[m*MX:(m+1)*MX], staging_register=0, mxu_index=m)
            pltpu.matmul_acc_lhs(oacc[m][0], wbn_ref[:, m*MX:(m+1)*MX], load_staged_rhs=0)
        bnext_ref[...] = (pltpu.matmul_pop(oacc[0][0]) + pltpu.matmul_pop(oacc[1][0])).astype(BF16)

    pl.run_scoped(body, *[pltpu.ACC(m)((KC, MX), F32) for m in range(2) for _ in range(NR)],
                  *[pltpu.ACC(m)((2*D, MX), F32) for m in range(2) for _ in range(OA)])

def attention(z, bias, mask, lnw, wqvt, wk2, bg, wo, bo, lnn, wbn, LAG=4, NR=5, OA=2, FD=3, FL={}):
    R, C, N = z.shape
    H = bias.shape[0]
    QB = MX
    full = lambda a: pl.BlockSpec(a.shape, lambda j: (0,)*a.ndim, pipeline_mode=pl.Buffered(1))
    return pl.pallas_call(
        functools.partial(fast_kernel, R, N, C, H, LAG, NR, OA, FD),
        grid=(N//QB,),
        in_specs=[full(z), pl.BlockSpec((H, N, QB), lambda j: (0, 0, j)), full(mask), full(lnw), full(wqvt), full(wk2),
                  full(bg), full(wo), full(bo), full(lnn), full(wbn)],
        out_specs=[pl.BlockSpec((R, C, QB), lambda j: (0, 0, j)), pl.BlockSpec((H*R, QB), lambda j: (0, j))],
        out_shape=[jax.ShapeDtypeStruct((R, C, N), BF16), jax.ShapeDtypeStruct((H*R, N), BF16)],
        scratch_shapes=[pltpu.VMEM((R, N, 2*C), BF16), pltpu.VMEM((R, 2*C, N), BF16), pltpu.VMEM((R, C, N), BF16),
                        pltpu.VMEM((R, C, N), F32), pltpu.VMEM((R, C, QB), BF16), pltpu.VMEM((R*C, QB), BF16),
                        pltpu.VMEM((H, N, QB), F32)],
        compiler_params=pltpu.CompilerParams(dimension_semantics=("arbitrary",), vmem_limit_bytes=48*2**20, flags=FL),
        name="att_fast",
    )(z, bias, mask, lnw, wqvt, wk2, bg, wo, bo, lnn, wbn)

def prep_weights(ln_w, w_in, b_g, w_b, w_o, b_o, R):
    C = w_o.shape[0]; H = w_b.shape[1]; D = C // H
    lnw = ln_w.astype(F32).T
    wq, wk, wv, wt = (w_in[:, i*C:(i+1)*C] for i in range(4))
    wqvt = jnp.pad(jnp.concatenate([wq, wv, wt], axis=1).T, ((0, MX-3*C), (0, MX-C)))
    wk2 = jnp.concatenate([wk.reshape(C, H, 1, D)]*2, axis=2).reshape(C, 2*C)
    wk2 = jnp.pad(wk2, ((0, MX-C), (0, MX-2*C)))
    bg = b_g.astype(F32).reshape(C, 1)
    bo = b_o.astype(F32).reshape(C, 1)
    eye = jnp.eye(R, dtype=w_b.dtype)
    wbn = (w_b.T[:, None, None, :] * eye[None, :, :, None]).reshape(H*R, R*C)
    wo = jnp.pad(w_o.T, ((0, 2*C-C), (0, MX-C)))
    return lnw, wqvt, wk2, bg, wo, bo, wbn


def safe_kernel(R, N, C, H, QB, KC,
               z_ref, bias_ref, mask_ref, lnw_ref, wqvt_ref, wk2_ref, bg_ref, wo_ref, bo_ref, lnn_ref, wbn_ref,
               out_ref, bnext_ref,
               k_s, q_s, v_s, g_s, o_s, y_s, bias_s, s_s):
    jb = pl.program_id(0)
    D = C // H

    @pl.when(jb == 0)
    def _():
        rows = lax.broadcasted_iota(jnp.int32, (16, N), 0)
        ones = jnp.where(rows == 0, 1.0, 0.0).astype(BF16)
        def prep(i, _):
            x = z_ref[i].astype(F32)
            y = _ln_t(x, lnw_ref[:, 0:1], lnw_ref[:, 1:2])
            p = jnp.dot(wqvt_ref[0:3*C, 0:C], y, preferred_element_type=F32)
            yt = y.T
            k2 = jnp.dot(yt, wk2_ref[0:C, 0:2*C], preferred_element_type=F32).astype(BF16)
            k_s[i] = k2
            q = p[0:C].astype(BF16).astype(F32) * (LOG2E * D ** -0.5)
            qh = q.astype(BF16)
            ql = (q - qh.astype(F32)).astype(BF16)
            v = p[C:2*C].astype(BF16)
            for h in range(H):
                q_s[i, 2*D*h:2*D*h+D] = qh[D*h:D*h+D]
                q_s[i, 2*D*h+D:2*D*h+2*D] = ql[D*h:D*h+D]
                v_s[i, h, 0:D] = v[D*h:D*h+D]
                v_s[i, h, D:2*D] = ones
            g_s[i] = jax.nn.sigmoid(p[2*C:3*C] + bg_ref[...])
            return 0
        lax.fori_loop(0, R, prep, 0)

    q0 = pl.multiple_of(jb * QB, QB)
    zero = jnp.zeros((2*D, QB), BF16)
    for h in range(H):
        for c in range(0, N, KC):
            bias_s[c:c+KC] = bias_ref[h, c:c+KC].astype(F32) * LOG2E + mask_ref[c:c+KC, 0:1]
        def row(i, _):
            qw = q_s[i, 2*D*h:2*D*(h+1), pl.ds(q0, QB)]
            w = jnp.concatenate([zero]*h + [qw] + [zero]*(H-1-h), axis=0)
            m = None
            for c in range(0, N, KC):
                s = jnp.dot(k_s[i, c:c+KC], w, preferred_element_type=F32) + bias_s[c:c+KC]
                s_s[c:c+KC] = s
                mc = jnp.max(s.reshape(KC//8, 8, QB), axis=0)
                m = mc if m is None else jnp.maximum(m, mc)
            m = jnp.max(m, axis=0, keepdims=True)
            acc = None
            for c in range(0, N, KC):
                e = jnp.exp2(s_s[c:c+KC] - m).astype(BF16)
                a = jnp.dot(v_s[i, h, :, c:c+KC], e, preferred_element_type=F32)
                acc = a if acc is None else acc + a
            o = acc[0:D] / acc[D:D+1]
            o_s[i, D*h:D*h+D] = (g_s[i, D*h:D*h+D, pl.ds(q0, QB)] * o).astype(BF16)
            return 0
        lax.fori_loop(0, R, row, 0)

    def fin(i, _):
        u = jnp.dot(wo_ref[0:C, 0:C], o_s[i], preferred_element_type=F32) + bo_ref[...]
        zn = (z_ref[i, :, pl.ds(q0, QB)].astype(F32) + u).astype(BF16)
        out_ref[i] = zn
        y_s[pl.ds(pl.multiple_of(i*C, C), C)] = _ln_t(zn.astype(F32), lnn_ref[:, 0:1], lnn_ref[:, 1:2])
        return 0
    lax.fori_loop(0, R, fin, 0)
    bnext_ref[...] = jnp.dot(wbn_ref[...], y_s[...], preferred_element_type=F32).astype(BF16)

def attention_safe(z, bias, mask, lnw, wqvt, wk2, bg, wo, bo, lnn, wbn, QB=256, KC=256):
    R, C, N = z.shape
    H = bias.shape[0]
    full = lambda a: pl.BlockSpec(a.shape, lambda j: (0,)*a.ndim, pipeline_mode=pl.Buffered(1))
    return pl.pallas_call(
        functools.partial(safe_kernel, R, N, C, H, QB, KC),
        grid=(N//QB,),
        in_specs=[full(z), pl.BlockSpec((H, N, QB), lambda j: (0, 0, j)), full(mask), full(lnw), full(wqvt), full(wk2),
                  full(bg), full(wo), full(bo), full(lnn), full(wbn)],
        out_specs=[pl.BlockSpec((R, C, QB), lambda j: (0, 0, j)), pl.BlockSpec((H*R, QB), lambda j: (0, j))],
        out_shape=[jax.ShapeDtypeStruct((R, C, N), BF16), jax.ShapeDtypeStruct((H*R, N), BF16)],
        scratch_shapes=[pltpu.VMEM((R, N, 2*C), BF16), pltpu.VMEM((R, 2*C, N), BF16), pltpu.VMEM((R, H, 2*(C//H), N), BF16),
                        pltpu.VMEM((R, C, N), F32), pltpu.VMEM((R, C, QB), BF16), pltpu.VMEM((R*C, QB), BF16),
                        pltpu.VMEM((N, QB), F32), pltpu.VMEM((N, QB), F32)],
        compiler_params=pltpu.CompilerParams(dimension_semantics=("arbitrary",), vmem_limit_bytes=60*2**20),
        name="att_safe",
    )(z, bias, mask, lnw, wqvt, wk2, bg, wo, bo, lnn, wbn)


def _ln_rows(x, w):
    x = x.astype(F32)
    mu = jnp.mean(x, axis=-1, keepdims=True)
    var = jnp.mean(jnp.square(x - mu), axis=-1, keepdims=True)
    y = (x - mu) * lax.rsqrt(var + EPS)
    return (y * w[0].astype(F32) + w[1].astype(F32)).astype(BF16)


def _safe_to_skip_max(ws):
    ln_w, w_in, b_g, w_b, w_o, b_o = (a.astype(F32) for a in ws)
    L, P, C, H = w_b.shape
    D = C // H
    g, b = ln_w[:, :, 0], ln_w[:, :, 1]
    w = w_in.reshape(L, P, C, 4, H, D)[:, :, :, 0:3]
    wg = w * g[:, :, :, None, None, None]
    gram = jnp.sum(wg[..., :, None] * wg[..., None, :], axis=2)
    gram2 = jnp.sum(gram[..., :, :, None] * gram[..., None, :, :], axis=-2)
    lam = jnp.sqrt(jnp.max(jnp.sum(jnp.abs(gram2), axis=-1), axis=-1))
    off = jnp.sqrt(jnp.sum(jnp.square(jnp.sum(w * b[:, :, :, None, None, None], axis=2)), axis=-1))
    n = (jnp.sqrt(lam) * C ** 0.5 + off) * 1.02
    nb = jnp.sqrt(jnp.sum(jnp.square(w_b * g[..., None]), axis=2)) * C ** 0.5 + jnp.abs(jnp.sum(w_b * b[..., None], axis=2))
    s = LOG2E * (n[:, :, 0] * n[:, :, 1] * D ** -0.5 + nb * 1.02)
    ok = (s <= 100.0) & (n[:, :, 2] <= 2.0 ** 14)
    return jnp.all(ok, axis=-1)


def solution(mesh):
    def local(zl, res_mask, ln_w, w_in, b_g, w_b, w_o, b_o):
        R, N, C = zl.shape
        H = w_b.shape[-1]
        G = N // R
        mask = jnp.broadcast_to(jnp.where(res_mask > 0, 0.0, NEG).astype(F32)[:, None], (N, 128))
        ws = (ln_w, w_in, b_g, w_b, w_o, b_o)
        ok = _safe_to_skip_max(ws)
        passes = [(l, p) for l in range(ln_w.shape[0]) for p in range(2)]
        sets = [prep_weights(*(a[l, p] for a in ws), R) for l, p in passes]

        y = _ln_rows(zl, ln_w[0, 0])
        b = jnp.einsum('jkc,ch->hjk', y, w_b[0, 0], preferred_element_type=F32).astype(BF16)
        bias = jnp.swapaxes(lax.all_gather(b, 'dap', axis=1, tiled=True), 1, 2)
        z = jnp.swapaxes(zl, 1, 2)
        for n, (l, p) in enumerate(passes):
            lnw, wqvt, wk2, bg, wo, bo, _ = sets[n]
            nxt = sets[(n+1) % len(sets)]
            z, bn = lax.cond(ok[l, p], attention, attention_safe, z, bias, mask, lnw, wqvt, wk2, bg, wo, bo, nxt[0], nxt[6])
            x = jnp.transpose(z.reshape(R, C, G, R), (2, 3, 0, 1))
            x = lax.all_to_all(x, 'dap', 0, 0, tiled=True)
            if n+1 < len(passes):
                bias = lax.all_gather(bn.reshape(H, R, N), 'dap', axis=1, tiled=True)
                z = jnp.transpose(x, (1, 3, 0, 2)).reshape(R, C, N)
        return jnp.transpose(x, (1, 0, 2, 3)).reshape(R, N, C)

    rows = P(('data', 'dap'))
    return jax.shard_map(local, mesh=mesh,
                         in_specs=(rows, P('data'), P(), P(), P(), P(), P(), P()),
                         out_specs=rows, check_vma=False)
```

time: 1550 us -> 789 us (0.51)
  matrix products: 649 us -> 1.15 us
  Pallas kernels: 0 us -> 267 us
  other arithmetic: 140 us -> 12.3 us
  blocking collectives: 148 us -> 24.9 us
  local copies, waits for them, and re-layouts: 229 us -> 118 us
  waiting for transfers between devices: 353 us -> 306 us
  starting transfers between devices: 0.25 us -> 31.1 us
    sub x6 -> x0, matrix products: 342 us -> none  [block(): p = jax.nn.softmax(s, axis=-1).astype(BF16)]
    dot_general x24 -> x1, matrix products: 307 us -> 1.15 us  [local(): jnp.einsum('jkc,ch->hjk', y, w_b[0, 0], preferred_element_type=F32)]
    pallas_call x0 -> x6, Pallas kernels: none -> 267 us  [attention(): pl.pallas_call(functools.partial(fast_kernel, R, N, C, H, LAG, NR, OA, FD...]
    all_gather x6, waiting for transfers between devices: 353 us -> 218 us  [the longest x5 156 us: local(): bias = lax.all_gather(bn.reshape(H, R, N), 'dap', axis=1, tiled=True)]
    all_to_all x6 -> x1, blocking collectives: 148 us -> 24.9 us  [local(): x = lax.all_to_all(x, 'dap', 0, 0, tiled=True)]
    add x6 -> x0, local copies, waits for them, and re-layouts: 115 us -> none  [_tri_start(): bias = jnp.transpose(b, (2, 0, 1)).astype(F32) + mask_bias]
    all_to_all x0 -> x5, waiting for transfers between devices: none -> 88.3 us  [local(): x = lax.all_to_all(x, 'dap', 0, 0, tiled=True)]
    add x6 -> x0, other arithmetic: 60.4 us -> none  [_tri_start(): bias = jnp.transpose(b, (2, 0, 1)).astype(F32) + mask_bias]
  transfers between devices with their start and end apart: 6 -> 11, of which waited for: 6 -> 11; matrix products, arithmetic and copies ran while one was open for 3% -> 10% of each run, Pallas kernels for 0% -> 0%
where the time goes in v1:
time: 789 us; the launch traced here: 781 us
  waiting for transfers between devices  306 us (39%)
  Pallas kernels  267 us (34%)
  local copies, waits for them, and re-layouts  118 us (15%)
  starting transfers between devices  31.1 us (4%)
  blocking collectives  24.9 us (3%)
  between operations  18.5 us (2%)
  other arithmetic  12.3 us (2%)
    pallas_call x6, Pallas kernels, attention(): pl.pallas_call(functools.partial(fast_kernel, R, N, C, H, LAG, NR, OA, FD...  267 us
    all_gather x5, waiting for transfers between devices, local(): bias = lax.all_gather(bn.reshape(H, R, N), 'dap', axis=1, tiled=True)  156 us
    all_to_all x5, waiting for transfers between devices, local(): x = lax.all_to_all(x, 'dap', 0, 0, tiled=True)  88.3 us
    unnamed x79, local copies, waits for them, and re-layouts  62.3 us
    all_gather x1, waiting for transfers between devices, local(): bias = jnp.swapaxes(lax.all_gather(b, 'dap', axis=1, tiled=True), 1, 2)  61.6 us
    all_to_all x5, starting transfers between devices, local(): x = lax.all_to_all(x, 'dap', 0, 0, tiled=True)  30.9 us
    another operation x36, local copies, waits for them, and re-layouts  28.7 us
    all_to_all x1, blocking collectives, local(): x = lax.all_to_all(x, 'dap', 0, 0, tiled=True)  24.9 us
  transfers between devices with their start and end apart: 11, of which 11 were waited for; matrix products, arithmetic and copies ran while one was open for 10% of the time, Pallas kernels for 0%

profile of v1, /device:TPU:1, one launch (start us, length us, event | category | flops | bytes accessed | tf_op | source)
XLA Modules:
  0.0 780.9 jit_solution(2328822384053459847)
XLA Ops:
  23.3 61.6 %all-gather.7.cloned.1.call-done = bf16[4,1024,1024]{2,0,1:T(4,128)(2,1)} async-done(((bf16[4,8,1024]{2,0,1:T(4,128)(2,1)}), bf16[4,1024,1024]{2,0,1:T(4,128)(2,1)}) %all-gather.7.cloned.1.call-update) | async-done | bytes 8388624 | tf_op jit(solution)/shard_map/all_gather | solution.py:298
  85.1 60.3 %conditional.6 = ((bf16[8,64,1024]{2,1,0:T(8,128)(2,1)}, bf16[32,1024]{1,0:T(8,128)(2,1)})) conditional(s32[]{:T(128)} %bitcast.10, (bf16[8,64,1024]{2,1,0:T(8,128)(2,1)S(1)}, bf16[4,1024,1024]{1,0,2:T(4,128)(2,1)}, f32[1024,128]{1,0:T(8,128)S(1)}, f32[64,2]{0,1:T(2,128)}, bf16[256,256]{1,0:T(8,128)(2,1)S(1)}, ...), branch_computations={%region_11.12_spmd, %region_12.13_spmd} | conditional | bytes 17042440 | solution.py:303
  85.3 13.7 %copy.458.bias_ref = bf16[4,1024,1024]{2,1,0:T(8,128)(2,1)} copy(bf16[4,1024,1024]{1,0,2:T(4,128)(2,1)} %get-tuple-element.966) | data formatting | bytes 16777216 | tf_op jit(solution)/shard_map
  100.8 44.5 %att_fast.6 = (bf16[8,64,1024]{2,1,0:T(8,128)(2,1)}, bf16[32,1024]{1,0:T(8,128)(2,1)}) custom-call(bf16[8,64,1024]{2,1,0:T(8,128)(2,1)S(1)} %get-tuple-element.283.z_ref, bf16[4,1024,1024]{2,1,0:T(8,128)(2,1)} %copy.458.bias_ref, f32[1024,128]{1,0:T(8,128)S(1)} %get-tuple-element.285.mask_ref, f32[64,2]{1,0:T(8,128)S(1)} %copy.459.lnw_ref, ...), custom_call_target="tpu_custom_call" | custom-call | tf_op jit(solution)/shard_map/cond/branch_1_fun/att_fast/pallas_call | solution.py:146
  154.0 6.0 all-to-all-start
  160.9 17.8 %all-to-all-done = bf16[128,2,2048]{2,1,0:T(2,128)(2,1)} async-done(((bf16[128,2,2048]{2,1,0:T(2,128)(2,1)}), bf16[128,2,2048]{2,1,0:T(2,128)(2,1)}, u32[]{:S(2)}, u32[]{:S(2)}) %all-to-all-start) | async-done | bytes 1048608 | tf_op jit(solution)/shard_map/all_to_all | solution.py:305
  183.1 31.3 %all-gather.9.cloned.1.call-done = bf16[4,1024,1024]{2,1,0:T(8,128)(2,1)} async-done(((bf16[4,8,1024]{2,1,0:T(8,128)(2,1)}), bf16[4,1024,1024]{2,1,0:T(8,128)(2,1)}) %all-gather.9.cloned.1.call-update) | async-done | bytes 8388624 | tf_op jit(solution)/shard_map/all_gather | solution.py:307
  214.4 49.1 %conditional.7 = ((bf16[8,64,1024]{2,1,0:T(8,128)(2,1)}, bf16[32,1024]{1,0:T(8,128)(2,1)})) conditional(s32[]{:T(128)} %bitcast.9, (bf16[8,64,1024]{1,2,0:T(8,128)(2,1)S(1)}, bf16[4,1024,1024]{2,1,0:T(8,128)(2,1)}, f32[1024,128]{1,0:T(8,128)S(1)}, f32[64,2]{0,1:T(2,128)}, bf16[256,256]{1,0:T(8,128)(2,1)S(1)}, ...), branch_computations={%region_13.14_spmd, %region_14.15_spmd} | conditional | bytes 6556708 | solution.py:303
  219.0 44.5 %att_fast.7 = (bf16[8,64,1024]{2,1,0:T(8,128)(2,1)}, bf16[32,1024]{1,0:T(8,128)(2,1)}) custom-call(bf16[8,64,1024]{2,1,0:T(8,128)(2,1)S(1)} %copy.477.z_ref, bf16[4,1024,1024]{2,1,0:T(8,128)(2,1)} %get-tuple-element.306.bias_ref, f32[1024,128]{1,0:T(8,128)S(1)} %get-tuple-element.307.mask_ref, f32[64,2]{1,0:T(8,128)S(1)} %copy.478.lnw_ref, ...), custom_call_target="tpu_custom_call" | custom-call | tf_op jit(solution)/shard_map/cond/branch_1_fun/att_fast/pallas_call | solution.py:146
  267.5 4.7 reshape.412
  272.2 6.2 all-to-all-start.1
  280.2 17.1 %all-to-all-done.1 = bf16[128,2,2048]{2,1,0:T(2,128)(2,1)} async-done(((bf16[128,2,2048]{2,1,0:T(2,128)(2,1)}), bf16[128,2,2048]{2,1,0:T(2,128)(2,1)}, u32[]{:S(2)}, u32[]{:S(2)}) %all-to-all-start.1) | async-done | bytes 1048608 | tf_op jit(solution)/shard_map/all_to_all | solution.py:305
  301.5 30.9 %all-gather.11.cloned.1.call-done = bf16[4,1024,1024]{2,1,0:T(8,128)(2,1)} async-done(((bf16[4,8,1024]{2,1,0:T(8,128)(2,1)}), bf16[4,1024,1024]{2,1,0:T(8,128)(2,1)}) %all-gather.11.cloned.1.call-update) | async-done | bytes 8388624 | tf_op jit(solution)/shard_map/all_gather | solution.py:307
  332.5 48.7 %conditional.8 = ((bf16[8,64,1024]{2,1,0:T(8,128)(2,1)}, bf16[32,1024]{1,0:T(8,128)(2,1)})) conditional(s32[]{:T(128)} %bitcast.8, (bf16[8,64,1024]{1,2,0:T(8,128)(2,1)S(1)}, bf16[4,1024,1024]{2,1,0:T(8,128)(2,1)}, f32[1024,128]{1,0:T(8,128)S(1)}, f32[64,2]{0,1:T(2,128)S(1)}, bf16[256,256]{1,0:T(8,128)(2,1)S(1)}, ...), branch_computations={%region_15.16_spmd, %region_16.17_spmd} | conditional | bytes 6556708 | solution.py:303
  336.6 44.5 %att_fast.8 = (bf16[8,64,1024]{2,1,0:T(8,128)(2,1)}, bf16[32,1024]{1,0:T(8,128)(2,1)}) custom-call(bf16[8,64,1024]{2,1,0:T(8,128)(2,1)S(1)} %copy.496.z_ref, bf16[4,1024,1024]{2,1,0:T(8,128)(2,1)} %get-tuple-element.328.bias_ref, f32[1024,128]{1,0:T(8,128)S(1)} %get-tuple-element.329.mask_ref, f32[64,2]{1,0:T(8,128)S(1)} %copy.497.lnw_ref, ...), custom_call_target="tpu_custom_call" | custom-call | tf_op jit(solution)/shard_map/cond/branch_1_fun/att_fast/pallas_call | solution.py:146
  385.1 4.7 reshape.414
  389.8 6.2 all-to-all-start.2
  397.1 17.7 %all-to-all-done.2 = bf16[128,2,2048]{2,1,0:T(2,128)(2,1)} async-done(((bf16[128,2,2048]{2,1,0:T(2,128)(2,1)}), bf16[128,2,2048]{2,1,0:T(2,128)(2,1)}, u32[]{:S(2)}, u32[]{:S(2)}) %all-to-all-start.2) | async-done | bytes 1048608 | tf_op jit(solution)/shard_map/all_to_all | solution.py:305
  419.1 31.0 %all-gather.13.cloned.1.call-done = bf16[4,1024,1024]{2,1,0:T(8,128)(2,1)} async-done(((bf16[4,8,1024]{2,1,0:T(8,128)(2,1)}), bf16[4,1024,1024]{2,1,0:T(8,128)(2,1)}) %all-gather.13.cloned.1.call-update) | async-done | bytes 8388624 | tf_op jit(solution)/shard_map/all_gather | solution.py:307
  450.2 48.4 %conditional.9 = ((bf16[8,64,1024]{2,1,0:T(8,128)(2,1)}, bf16[32,1024]{1,0:T(8,128)(2,1)})) conditional(s32[]{:T(128)} %bitcast.7, (bf16[8,64,1024]{1,2,0:T(8,128)(2,1)S(1)}, bf16[4,1024,1024]{2,1,0:T(8,128)(2,1)}, f32[1024,128]{1,0:T(8,128)S(1)}, f32[64,2]{0,1:T(2,128)S(1)}, bf16[256,256]{1,0:T(8,128)(2,1)S(1)}, ...), branch_computations={%region_17.18_spmd, %region_18.19_spmd} | conditional | bytes 6556708 | solution.py:303
  454.1 44.5 %att_fast.9 = (bf16[8,64,1024]{2,1,0:T(8,128)(2,1)}, bf16[32,1024]{1,0:T(8,128)(2,1)}) custom-call(bf16[8,64,1024]{2,1,0:T(8,128)(2,1)S(1)} %copy.515.z_ref, bf16[4,1024,1024]{2,1,0:T(8,128)(2,1)} %get-tuple-element.350.bias_ref, f32[1024,128]{1,0:T(8,128)S(1)} %get-tuple-element.351.mask_ref, f32[64,2]{1,0:T(8,128)S(1)} %copy.516.lnw_ref, ...), custom_call_target="tpu_custom_call" | custom-call | tf_op jit(solution)/shard_map/cond/branch_1_fun/att_fast/pallas_call | solution.py:146
  507.2 6.2 all-to-all-start.3
  514.4 17.9 %all-to-all-done.3 = bf16[128,2,2048]{2,1,0:T(2,128)(2,1)} async-done(((bf16[128,2,2048]{2,1,0:T(2,128)(2,1)}), bf16[128,2,2048]{2,1,0:T(2,128)(2,1)}, u32[]{:S(2)}, u32[]{:S(2)}) %all-to-all-start.3) | async-done | bytes 1048608 | tf_op jit(solution)/shard_map/all_to_all | solution.py:305
  536.6 31.3 %all-gather.15.cloned.1.call-done = bf16[4,1024,1024]{2,1,0:T(8,128)(2,1)} async-done(((bf16[4,8,1024]{2,1,0:T(8,128)(2,1)}), bf16[4,1024,1024]{2,1,0:T(8,128)(2,1)}) %all-gather.15.cloned.1.call-update) | async-done | bytes 8388624 | tf_op jit(solution)/shard_map/all_gather | solution.py:307
  567.9 48.5 %conditional.10 = ((bf16[8,64,1024]{2,1,0:T(8,128)(2,1)}, bf16[32,1024]{1,0:T(8,128)(2,1)})) conditional(s32[]{:T(128)} %bitcast.6, (bf16[8,64,1024]{1,2,0:T(8,128)(2,1)S(1)}, bf16[4,1024,1024]{2,1,0:T(8,128)(2,1)}, f32[1024,128]{1,0:T(8,128)S(1)}, f32[64,2]{0,1:T(2,128)S(1)}, bf16[256,256]{1,0:T(8,128)(2,1)S(1)}, ...), branch_computations={%region_19.20_spmd, %region_20.21_spmd} | conditional | bytes 6556708 | solution.py:303
  571.8 44.5 %att_fast.10 = (bf16[8,64,1024]{2,1,0:T(8,128)(2,1)}, bf16[32,1024]{1,0:T(8,128)(2,1)}) custom-call(bf16[8,64,1024]{2,1,0:T(8,128)(2,1)S(1)} %copy.534.z_ref, bf16[4,1024,1024]{2,1,0:T(8,128)(2,1)} %get-tuple-element.372.bias_ref, f32[1024,128]{1,0:T(8,128)S(1)} %get-tuple-element.373.mask_ref, f32[64,2]{1,0:T(8,128)S(1)} %copy.535.lnw_ref, ...), custom_call_target="tpu_custom_call" | custom-call | tf_op jit(solution)/shard_map/cond/branch_1_fun/att_fast/pallas_call | solution.py:146
  625.0 6.2 all-to-all-start.4
  632.2 17.8 %all-to-all-done.4 = bf16[128,2,2048]{2,1,0:T(2,128)(2,1)} async-done(((bf16[128,2,2048]{2,1,0:T(2,128)(2,1)}), bf16[128,2,2048]{2,1,0:T(2,128)(2,1)}, u32[]{:S(2)}, u32[]{:S(2)}) %all-to-all-start.4) | async-done | bytes 1048608 | tf_op jit(solution)/shard_map/all_to_all | solution.py:305
  654.3 31.3 %all-gather.17.cloned.1.call-done = bf16[4,1024,1024]{2,1,0:T(8,128)(2,1)} async-done(((bf16[4,8,1024]{2,1,0:T(8,128)(2,1)}), bf16[4,1024,1024]{2,1,0:T(8,128)(2,1)}) %all-gather.17.cloned.1.call-update) | async-done | bytes 8388624 | tf_op jit(solution)/shard_map/all_gather | solution.py:307
  685.7 49.2 %conditional.11 = (bf16[8,64,1024]{2,1,0:T(8,128)(2,1)}) conditional(s32[]{:T(128)} %bitcast.5, (bf16[8,64,1024]{1,2,0:T(8,128)(2,1)S(1)}, bf16[4,1024,1024]{2,1,0:T(8,128)(2,1)}, f32[1024,128]{1,0:T(8,128)S(1)}, f32[64,2]{0,1:T(2,128)S(1)}, bf16[256,256]{1,0:T(8,128)(2,1)S(1)}, /*index=5*/bf16[256,256]{0,1:T(8,128)(2,1)S(1)}, ...), branch_computations={%region_21.22_spmd, %region_22.23_spmd} | conditional | bytes 6556708 | solution.py:303
  690.3 44.5 %att_fast.11 = (bf16[8,64,1024]{2,1,0:T(8,128)(2,1)}, bf16[32,1024]{1,0:T(8,128)(2,1)}) custom-call(bf16[8,64,1024]{2,1,0:T(8,128)(2,1)S(1)} %copy.553.z_ref, bf16[4,1024,1024]{2,1,0:T(8,128)(2,1)} %get-tuple-element.395.bias_ref, f32[1024,128]{1,0:T(8,128)S(1)} %get-tuple-element.396.mask_ref, f32[64,2]{1,0:T(8,128)S(1)} %copy.554.lnw_ref, ...), custom_call_target="tpu_custom_call" | custom-call | tf_op jit(solution)/shard_map/cond/branch_1_fun/att_fast/pallas_call | solution.py:146
  742.7 24.9 %all_to_all.30 = bf16[128,2,2048]{2,1,0:T(2,128)(2,1)} all-to-all(bf16[128,2,2048]{2,1,0:T(2,128)(2,1)S(1)} %reshape.420), channel_id=1, replica_groups=mesh['data'=1,'dap'=128] {'dap'}, dimensions={0} | all-to-all | bytes 2097152 | tf_op jit(solution)/shard_map/all_to_all | solution.py:305
  (222 shorter events, 108.7 us)
Async XLA Ops:
  6.5 78.4 %all-gather.7.cloned.1.call-start = ((), (), s32[]{:S(2)}) async-start(), calls=%async_computation.6 | async-start | bytes 8454144 | tf_op jit(solution)/shard_map/all_gather | solution.py:298
  11.6 202.8 %all-gather.9.cloned.1.call-start = ((), (), s32[]{:S(2)}) async-start(), calls=%async_computation.7 | async-start | bytes 8454144 | tf_op jit(solution)/shard_map/all_gather | solution.py:307
  14.7 7.9 %copy-start.19 = (bf16[3,2,64]{2,1,0:T(2,128)(2,1)S(1)}, bf16[3,2,64]{2,1,0:T(2,128)(2,1)}, u32[]{:S(2)}) copy-start(bf16[3,2,64]{2,1,0:T(2,128)(2,1)} %param.27) | copy-start | bytes 2308
  14.7 7.9 %copy-start.20 = (bf16[3,2,64]{2,1,0:T(2,128)(2,1)S(1)}, bf16[3,2,64]{2,1,0:T(2,128)(2,1)}, u32[]{:S(2)}) copy-start(bf16[3,2,64]{2,1,0:T(2,128)(2,1)} %param.24) | copy-start | bytes 2308
  14.7 8.6 %copy-start.31 = (s32[1024]{0:T(1024)S(1)}, s32[1024]{0:T(1024)}, u32[]{:S(2)}) copy-start(s32[1024]{0:T(1024)} %param.21) | copy-start | bytes 12292
  154.0 24.8 %all-to-all-start = ((bf16[128,2,2048]{2,1,0:T(2,128)(2,1)}), bf16[128,2,2048]{2,1,0:T(2,128)(2,1)}, u32[]{:S(2)}, u32[]{:S(2)}) async-start(bf16[128,2,2048]{2,1,0:T(2,128)(2,1)} %reshape.410), calls=%async_computation | async-start | bytes 2097152 | tf_op jit(solution)/shard_map/all_to_all | solution.py:305
  160.0 172.5 %all-gather.11.cloned.1.call-start = ((), (), s32[]{:S(2)}) async-start(), calls=%async_computation.8 | async-start | bytes 8454144 | tf_op jit(solution)/shard_map/all_gather | solution.py:307
  182.8 31.6 %copy-start.16 = (f32[64,2]{0,1:T(2,128)S(1)}, f32[64,2]{0,1:T(2,128)}, u32[]{:S(2)}) copy-start(f32[64,2]{0,1:T(2,128)} %get-tuple-element.1122) | copy-start | bytes 1540
  182.8 31.6 %copy-start.29 = (f32[64,1]{0,1:T(1,128)S(1)}, f32[64,1]{0,1:T(1,128)}, u32[]{:S(2)}) copy-start(f32[64,1]{0,1:T(1,128)} %get-tuple-element.1139) | copy-start | bytes 772
  182.8 31.6 %copy-start.30 = (f32[64,1]{0,1:T(1,128)S(1)}, f32[64,1]{0,1:T(1,128)}, u32[]{:S(2)}) copy-start(f32[64,1]{0,1:T(1,128)} %get-tuple-element.1162) | copy-start | bytes 772
  267.5 11.7 %copy-start.6 = (bf16[64,256]{0,1:T(8,128)(2,1)S(1)}, bf16[64,256]{0,1:T(8,128)(2,1)}, u32[]{:S(2)}) copy-start(bf16[64,256]{0,1:T(8,128)(2,1)} %get-tuple-element.1091) | copy-start | bytes 98308
  272.2 25.1 %all-to-all-start.1 = ((bf16[128,2,2048]{2,1,0:T(2,128)(2,1)}), bf16[128,2,2048]{2,1,0:T(2,128)(2,1)}, u32[]{:S(2)}, u32[]{:S(2)}) async-start(bf16[128,2,2048]{2,1,0:T(2,128)(2,1)} %reshape.412), calls=%async_computation.1 | async-start | bytes 2097152 | tf_op jit(solution)/shard_map/all_to_all | solution.py:305
  278.4 171.7 %all-gather.13.cloned.1.call-start = ((), (), s32[]{:S(2)}) async-start(), calls=%async_computation.9 | async-start | bytes 8454144 | tf_op jit(solution)/shard_map/all_gather | solution.py:307
  301.2 31.2 %copy-start.15 = (f32[64,2]{0,1:T(2,128)S(1)}, f32[64,2]{0,1:T(2,128)}, u32[]{:S(2)}) copy-start(f32[64,2]{0,1:T(2,128)} %get-tuple-element.1121) | copy-start | bytes 1540
  301.2 31.2 %copy-start.17 = (f32[64,2]{0,1:T(2,128)S(1)}, f32[64,2]{0,1:T(2,128)}, u32[]{:S(2)}) copy-start(f32[64,2]{0,1:T(2,128)} %get-tuple-element.1122) | copy-start | bytes 1540
  301.2 31.2 %copy-start.27 = (f32[64,1]{0,1:T(1,128)S(1)}, f32[64,1]{0,1:T(1,128)}, u32[]{:S(2)}) copy-start(f32[64,1]{0,1:T(1,128)} %get-tuple-element.1138) | copy-start | bytes 772
  301.2 31.2 %copy-start.28 = (f32[64,1]{0,1:T(1,128)S(1)}, f32[64,1]{0,1:T(1,128)}, u32[]{:S(2)}) copy-start(f32[64,1]{0,1:T(1,128)} %get-tuple-element.1163) | copy-start | bytes 772
  385.1 11.7 %copy-start.11 = (bf16[64,64]{0,1:T(8,128)(2,1)S(1)}, bf16[64,64]{0,1:T(8,128)(2,1)}, u32[]{:S(2)}) copy-start(bf16[64,64]{0,1:T(8,128)(2,1)} %get-tuple-element.1107) | copy-start | bytes 24580
  385.1 11.7 %copy-start.10 = (bf16[64,64]{0,1:T(8,128)(2,1)S(1)}, bf16[64,64]{0,1:T(8,128)(2,1)}, u32[]{:S(2)}) copy-start(bf16[64,64]{0,1:T(8,128)(2,1)} %get-tuple-element.1106) | copy-start | bytes 24580
  389.8 25.1 %all-to-all-start.2 = ((bf16[128,2,2048]{2,1,0:T(2,128)(2,1)}), bf16[128,2,2048]{2,1,0:T(2,128)(2,1)}, u32[]{:S(2)}, u32[]{:S(2)}) async-start(bf16[128,2,2048]{2,1,0:T(2,128)(2,1)} %reshape.414), calls=%async_computation.2 | async-start | bytes 2097152 | tf_op jit(solution)/shard_map/all_to_all | solution.py:305
  396.1 171.8 %all-gather.15.cloned.1.call-start = ((), (), s32[]{:S(2)}) async-start(), calls=%async_computation.10 | async-start | bytes 8454144 | tf_op jit(solution)/shard_map/all_gather | solution.py:307
  418.8 31.4 %copy-start.14 = (f32[64,2]{0,1:T(2,128)S(1)}, f32[64,2]{0,1:T(2,128)}, u32[]{:S(2)}) copy-start(f32[64,2]{0,1:T(2,128)} %get-tuple-element.1125) | copy-start | bytes 1540
  418.8 31.3 %copy-start.25 = (f32[64,1]{0,1:T(1,128)S(1)}, f32[64,1]{0,1:T(1,128)}, u32[]{:S(2)}) copy-start(f32[64,1]{0,1:T(1,128)} %get-tuple-element.1137) | copy-start | bytes 772
  418.9 31.3 %copy-start.26 = (f32[64,1]{0,1:T(1,128)S(1)}, f32[64,1]{0,1:T(1,128)}, u32[]{:S(2)}) copy-start(f32[64,1]{0,1:T(1,128)} %get-tuple-element.1164) | copy-start | bytes 772
  507.2 25.1 %all-to-all-start.3 = ((bf16[128,2,2048]{2,1,0:T(2,128)(2,1)}), bf16[128,2,2048]{2,1,0:T(2,128)(2,1)}, u32[]{:S(2)}, u32[]{:S(2)}) async-start(bf16[128,2,2048]{2,1,0:T(2,128)(2,1)} %reshape.416), calls=%async_computation.3 | async-start | bytes 2097152 | tf_op jit(solution)/shard_map/all_to_all | solution.py:305
  513.5 172.2 %all-gather.17.cloned.1.call-start = ((), (), s32[]{:S(2)}) async-start(), calls=%async_computation.11 | async-start | bytes 8454144 | tf_op jit(solution)/shard_map/all_gather | solution.py:307
  536.3 31.6 %copy-start.13 = (f32[64,2]{0,1:T(2,128)S(1)}, f32[64,2]{0,1:T(2,128)}, u32[]{:S(2)}) copy-start(f32[64,2]{0,1:T(2,128)} %get-tuple-element.1120) | copy-start | bytes 1540
  536.3 31.6 %copy-start.23 = (f32[64,1]{0,1:T(1,128)S(1)}, f32[64,1]{0,1:T(1,128)}, u32[]{:S(2)}) copy-start(f32[64,1]{0,1:T(1,128)} %get-tuple-element.1141) | copy-start | bytes 772
  536.3 31.6 %copy-start.24 = (f32[64,1]{0,1:T(1,128)S(1)}, f32[64,1]{0,1:T(1,128)}, u32[]{:S(2)}) copy-start(f32[64,1]{0,1:T(1,128)} %get-tuple-element.1160) | copy-start | bytes 772
  625.0 25.0 %all-to-all-start.4 = ((bf16[128,2,2048]{2,1,0:T(2,128)(2,1)}), bf16[128,2,2048]{2,1,0:T(2,128)(2,1)}, u32[]{:S(2)}, u32[]{:S(2)}) async-start(bf16[128,2,2048]{2,1,0:T(2,128)(2,1)} %reshape.418), calls=%async_computation.4 | async-start | bytes 2097152 | tf_op jit(solution)/shard_map/all_to_all | solution.py:305
  654.0 31.6 %copy-start.21 = (f32[64,1]{0,1:T(1,128)S(1)}, f32[64,1]{0,1:T(1,128)}, u32[]{:S(2)}) copy-start(f32[64,1]{0,1:T(1,128)} %get-tuple-element.1136) | copy-start | bytes 772
  654.0 31.6 %copy-start.22 = (f32[64,1]{0,1:T(1,128)S(1)}, f32[64,1]{0,1:T(1,128)}, u32[]{:S(2)}) copy-start(f32[64,1]{0,1:T(1,128)} %get-tuple-element.1165) | copy-start | bytes 772
  (11 other events, 34.5 us)
Sparse Core Ops, SparseCore 0:
  11.7 73.1 all-gather.6
  145.5 68.8 all-gather.8
  263.7 68.7 all-gather.10
  381.3 68.8 all-gather.12
  498.8 69.0 all-gather.14
  616.5 69.0 all-gather.16

commit v2 on v1

--- a/solution.py
+++ b/solution.py
@@ -18,11 +18,22 @@
 def fast_kernel(R, N, C, H, LAG, NR, OA, FD,
                z_ref, bias_ref, mask_ref, lnw_ref, wqvt_ref, wk2_ref, bg_ref, wo_ref, bo_ref, lnn_ref, wbn_ref,
                out_ref, bnext_ref,
-               k_s, q_s, v_s, g_s, o_s, y_s, bias_s):
+               k_s, q_s, v_s, g_s, o_s, y_s, bias_s, x_s, zt_s, send_sem, recv_sem, own_sem):
     jb = pl.program_id(0)
+    me = lax.axis_index('dap')
+    n_dev = lax.axis_size('dap')
     D = C // H
     QB = MX
     KC = 128
+
+    @pl.when(jb == 0)
+    def _():
+        barrier = pltpu.get_barrier_semaphore()
+        def greet(k, _):
+            pl.semaphore_signal(barrier, inc=1, device_id={'dap': lax.rem(me + k, n_dev)}, device_id_type=pl.DeviceIdType.MESH)
+            return 0
+        lax.fori_loop(1, n_dev, greet, 0)
+        pl.semaphore_wait(barrier, n_dev - 1)
     CH = N // KC
     q0 = pl.multiple_of(jb * QB, QB)
 
@@ -126,14 +137,33 @@
                 i = 2*t+m
                 u = pltpu.matmul_pop(sacc[m][0])[0:C] + bo_ref[...]
                 zn = (z_ref[i, :, pl.ds(q0, QB)].astype(F32) + u).astype(BF16)
-                out_ref[i] = zn
+                zt_s[pl.ds(pl.multiple_of(i*C, C), C)] = zn
                 y_s[pl.ds(pl.multiple_of(i*C, C), C)] = _ln_t(zn.astype(F32), lnn_ref[:, 0:1], lnn_ref[:, 1:2])
             return 0
         lax.fori_loop(0, R//2, upd, 0)
+        x_s[pl.ds(jb * (QB//R), QB//R)] = zt_s[...].T.reshape(QB//R, R, R*C)
         for m in range(2):
             pltpu.matmul_push_rhs(y_s[m*MX:(m+1)*MX], staging_register=0, mxu_index=m)
             pltpu.matmul_acc_lhs(oacc[m][0], wbn_ref[:, m*MX:(m+1)*MX], load_staged_rhs=0)
         bnext_ref[...] = (pltpu.matmul_pop(oacc[0][0]) + pltpu.matmul_pop(oacc[1][0])).astype(BF16)
+
+        def send(k, _):
+            d = jb * (QB//R) + k
+            @pl.when(d != me)
+            def _():
+                pltpu.make_async_remote_copy(x_s.at[d], out_ref.at[me], send_sem, recv_sem,
+                                             device_id={'dap': d}, device_id_type=pl.DeviceIdType.MESH).start()
+            @pl.when(d == me)
+            def _():
+                pltpu.make_async_copy(x_s.at[d], out_ref.at[d], own_sem).start()
+            return 0
+        lax.fori_loop(0, QB//R, send, 0)
+
+        @pl.when(jb == pl.num_programs(0) - 1)
+        def _():
+            pltpu.make_async_copy(x_s.at[0], out_ref.at[0], own_sem).wait()
+            pltpu.make_async_copy(x_s.at[pl.ds(0, n_dev-1)], out_ref.at[pl.ds(0, n_dev-1)], send_sem).wait()
+            pltpu.make_async_copy(x_s.at[pl.ds(0, n_dev-1)], out_ref.at[pl.ds(0, n_dev-1)], recv_sem).wait()
 
     pl.run_scoped(body, *[pltpu.ACC(m)((KC, MX), F32) for m in range(2) for _ in range(NR)],
                   *[pltpu.ACC(m)((2*D, MX), F32) for m in range(2) for _ in range(OA)])
@@ -148,12 +178,13 @@
         grid=(N//QB,),
         in_specs=[full(z), pl.BlockSpec((H, N, QB), lambda j: (0, 0, j)), full(mask), full(lnw), full(wqvt), full(wk2),
                   full(bg), full(wo), full(bo), full(lnn), full(wbn)],
-        out_specs=[pl.BlockSpec((R, C, QB), lambda j: (0, 0, j)), pl.BlockSpec((H*R, QB), lambda j: (0, j))],
-        out_shape=[jax.ShapeDtypeStruct((R, C, N), BF16), jax.ShapeDtypeStruct((H*R, N), BF16)],
+        out_specs=[pl.BlockSpec(memory_space=pl.ANY), pl.BlockSpec((H*R, QB), lambda j: (0, j))],
+        out_shape=[jax.ShapeDtypeStruct((N//R, R, R*C), BF16), jax.ShapeDtypeStruct((H*R, N), BF16)],
         scratch_shapes=[pltpu.VMEM((R, N, 2*C), BF16), pltpu.VMEM((R, 2*C, N), BF16), pltpu.VMEM((R, C, N), BF16),
                         pltpu.VMEM((R, C, N), F32), pltpu.VMEM((R, C, QB), BF16), pltpu.VMEM((R*C, QB), BF16),
-                        pltpu.VMEM((H, N, QB), F32)],
-        compiler_params=pltpu.CompilerParams(dimension_semantics=("arbitrary",), vmem_limit_bytes=48*2**20, flags=FL),
+                        pltpu.VMEM((H, N, QB), F32), pltpu.VMEM((N//R, R, R*C), BF16), pltpu.VMEM((R*C, QB), BF16),
+                        pltpu.SemaphoreType.DMA, pltpu.SemaphoreType.DMA, pltpu.SemaphoreType.DMA],
+        compiler_params=pltpu.CompilerParams(dimension_semantics=("arbitrary",), vmem_limit_bytes=48*2**20, flags=FL, collective_id=0, has_side_effects=True),
         name="att_fast",
     )(z, bias, mask, lnw, wqvt, wk2, bg, wo, bo, lnn, wbn)
 
@@ -175,8 +206,19 @@
 def safe_kernel(R, N, C, H, QB, KC,
                z_ref, bias_ref, mask_ref, lnw_ref, wqvt_ref, wk2_ref, bg_ref, wo_ref, bo_ref, lnn_ref, wbn_ref,
                out_ref, bnext_ref,
-               k_s, q_s, v_s, g_s, o_s, y_s, bias_s, s_s):
+               k_s, q_s, v_s, g_s, o_s, y_s, bias_s, s_s, x_s, zt_s, send_sem, recv_sem, own_sem):
     jb = pl.program_id(0)
+    me = lax.axis_index('dap')
+    n_dev = lax.axis_size('dap')
+
+    @pl.when(jb == 0)
+    def _():
+        barrier = pltpu.get_barrier_semaphore()
+        def greet(k, _):
+            pl.semaphore_signal(barrier, inc=1, device_id={'dap': lax.rem(me + k, n_dev)}, device_id_type=pl.DeviceIdType.MESH)
+            return 0
+        lax.fori_loop(1, n_dev, greet, 0)
+        pl.semaphore_wait(barrier, n_dev - 1)
     D = C // H
 
     @pl.when(jb == 0)
@@ -231,11 +273,31 @@
     def fin(i, _):
         u = jnp.dot(wo_ref[0:C, 0:C], o_s[i], preferred_element_type=F32) + bo_ref[...]
         zn = (z_ref[i, :, pl.ds(q0, QB)].astype(F32) + u).astype(BF16)
-        out_ref[i] = zn
+        zt_s[pl.ds(pl.multiple_of(i*C, C), C)] = zn
         y_s[pl.ds(pl.multiple_of(i*C, C), C)] = _ln_t(zn.astype(F32), lnn_ref[:, 0:1], lnn_ref[:, 1:2])
         return 0
     lax.fori_loop(0, R, fin, 0)
     bnext_ref[...] = jnp.dot(wbn_ref[...], y_s[...], preferred_element_type=F32).astype(BF16)
+    x_s[pl.ds(jb * (QB//R), QB//R)] = zt_s[...].T.reshape(QB//R, R, R*C)
+
+    def send(k, _):
+        d = jb * (QB//R) + k
+        @pl.when(d != me)
+        def _():
+            pltpu.make_async_remote_copy(x_s.at[d], out_ref.at[me], send_sem, recv_sem,
+                                         device_id={'dap': d}, device_id_type=pl.DeviceIdType.MESH).start()
+        @pl.when(d == me)
+        def _():
+            pltpu.make_async_copy(x_s.at[d], out_ref.at[d], own_sem).start()
+        return 0
+    lax.fori_loop(0, QB//R, send, 0)
+
+    @pl.when(jb == pl.num_programs(0) - 1)
+    def _():
+        pltpu.make_async_copy(x_s.at[0], out_ref.at[0], own_sem).wait()
+        pltpu.make_async_copy(x_s.at[pl.ds(0, n_dev-1)], out_ref.at[pl.ds(0, n_dev-1)], send_sem).wait()
+        pltpu.make_async_copy(x_s.at[pl.ds(0, n_dev-1)], out_ref.at[pl.ds(0, n_dev-1)], recv_sem).wait()
+
 
 def attention_safe(z, bias, mask, lnw, wqvt, wk2, bg, wo, bo, lnn, wbn, QB=256, KC=256):
     R, C, N = z.shape
@@ -246,12 +308,13 @@
         grid=(N//QB,),
         in_specs=[full(z), pl.BlockSpec((H, N, QB), lambda j: (0, 0, j)), full(mask), full(lnw), full(wqvt), full(wk2),
                   full(bg), full(wo), full(bo), full(lnn), full(wbn)],
-        out_specs=[pl.BlockSpec((R, C, QB), lambda j: (0, 0, j)), pl.BlockSpec((H*R, QB), lambda j: (0, j))],
-        out_shape=[jax.ShapeDtypeStruct((R, C, N), BF16), jax.ShapeDtypeStruct((H*R, N), BF16)],
+        out_specs=[pl.BlockSpec(memory_space=pl.ANY), pl.BlockSpec((H*R, QB), lambda j: (0, j))],
+        out_shape=[jax.ShapeDtypeStruct((N//R, R, R*C), BF16), jax.ShapeDtypeStruct((H*R, N), BF16)],
         scratch_shapes=[pltpu.VMEM((R, N, 2*C), BF16), pltpu.VMEM((R, 2*C, N), BF16), pltpu.VMEM((R, H, 2*(C//H), N), BF16),
                         pltpu.VMEM((R, C, N), F32), pltpu.VMEM((R, C, QB), BF16), pltpu.VMEM((R*C, QB), BF16),
-                        pltpu.VMEM((N, QB), F32), pltpu.VMEM((N, QB), F32)],
-        compiler_params=pltpu.CompilerParams(dimension_semantics=("arbitrary",), vmem_limit_bytes=60*2**20),
+                        pltpu.VMEM((N, QB), F32), pltpu.VMEM((N, QB), F32), pltpu.VMEM((N//R, R, R*C), BF16), pltpu.VMEM((R*C, QB), BF16),
+                        pltpu.SemaphoreType.DMA, pltpu.SemaphoreType.DMA, pltpu.SemaphoreType.DMA],
+        compiler_params=pltpu.CompilerParams(dimension_semantics=("arbitrary",), vmem_limit_bytes=60*2**20, collective_id=0, has_side_effects=True),
         name="att_safe",
     )(z, bias, mask, lnw, wqvt, wk2, bg, wo, bo, lnn, wbn)
 
@@ -293,6 +356,11 @@
         passes = [(l, p) for l in range(ln_w.shape[0]) for p in range(2)]
         sets = [prep_weights(*(a[l, p] for a in ws), R) for l, p in passes]
 
+        def safe(*args):
+            z, bn = attention_safe(*args)
+            x = jnp.transpose(z.reshape(R, C, G, R), (2, 3, 0, 1)).reshape(G, R, R*C)
+            return lax.all_to_all(x, 'dap', 0, 0, tiled=True), bn
+
         y = _ln_rows(zl, ln_w[0, 0])
         b = jnp.einsum('jkc,ch->hjk', y, w_b[0, 0], preferred_element_type=F32).astype(BF16)
         bias = jnp.swapaxes(lax.all_gather(b, 'dap', axis=1, tiled=True), 1, 2)
@@ -300,9 +368,8 @@
         for n, (l, p) in enumerate(passes):
             lnw, wqvt, wk2, bg, wo, bo, _ = sets[n]
             nxt = sets[(n+1) % len(sets)]
-            z, bn = lax.cond(ok[l, p], attention, attention_safe, z, bias, mask, lnw, wqvt, wk2, bg, wo, bo, nxt[0], nxt[6])
-            x = jnp.transpose(z.reshape(R, C, G, R), (2, 3, 0, 1))
-            x = lax.all_to_all(x, 'dap', 0, 0, tiled=True)
+            x, bn = attention_safe(z, bias, mask, lnw, wqvt, wk2, bg, wo, bo, nxt[0], nxt[6])
+            x = x.reshape(G, R, R, C)
             if n+1 < len(passes):
                 bias = lax.all_gather(bn.reshape(H, R, N), 'dap', axis=1, tiled=True)
                 z = jnp.transpose(x, (1, 3, 0, 2)).reshape(R, C, N)

time: 789 us -> 1110 us (1.41)
  Pallas kernels: 267 us -> 642 us
  waiting for transfers between devices: 306 us -> 370 us
  local copies, waits for them, and re-layouts: 118 us -> 74.5 us
  starting transfers between devices: 31.1 us -> 0.61 us
  blocking collectives: 24.9 us -> 0 us
    pallas_call x6, Pallas kernels: 267 us -> 642 us  [attention_safe(): pl.pallas_call(functools.partial(safe_kernel, R, N, C, H, QB, KC), grid=(...]
    all_gather x5, waiting for transfers between devices: 156 us -> 305 us  [local(): bias = lax.all_gather(bn.reshape(H, R, N), 'dap', axis=1, tiled=True)]
    all_to_all x5 -> x0, waiting for transfers between devices: 88.3 us -> none  [local(): x = lax.all_to_all(x, 'dap', 0, 0, tiled=True)]
    unnamed x79 -> x56, local copies, waits for them, and re-layouts: 62.3 us -> 1.31 us
    all_to_all x5 -> x0, starting transfers between devices: 30.9 us -> none  [local(): x = lax.all_to_all(x, 'dap', 0, 0, tiled=True)]
    another operation x36 -> x0, local copies, waits for them, and re-layouts: 28.7 us -> none
    all_to_all x1 -> x0, blocking collectives: 24.9 us -> none  [local(): x = lax.all_to_all(x, 'dap', 0, 0, tiled=True)]
    cond x16 -> x0, local copies, waits for them, and re-layouts: 18.7 us -> none  [the longest x6 12.1 us: local(): lax.cond(ok[l, p], attention, attention_safe, z, bias, mask, lnw, wqvt, w...]
  transfers between devices with their start and end apart: 11 -> 6, of which waited for: 11 -> 6; matrix products, arithmetic and copies ran while one was open for 10% -> 5% of each run, Pallas kernels for 0% -> 0%
where the time goes in v2:
time: 1110 us
  Pallas kernels  642 us (58%)
  waiting for transfers between devices  370 us (33%)
  local copies, waits for them, and re-layouts  74.5 us (7%)
  between operations  14 us (1%)
    pallas_call x6, Pallas kernels, attention_safe(): pl.pallas_call(functools.partial(safe_kernel, R, N, C, H, QB, KC), grid=(...  642 us
    all_gather x5, waiting for transfers between devices, local(): bias = lax.all_gather(bn.reshape(H, R, N), 'dap', axis=1, tiled=True)  305 us
    all_gather x1, waiting for transfers between devices, local(): bias = jnp.swapaxes(lax.all_gather(b, 'dap', axis=1, tiled=True), 1, 2)  64.8 us
  transfers between devices with their start and end apart: 6, of which 6 were waited for; matrix products, arithmetic and copies ran while one was open for 5% of the time, Pallas kernels for 0%

profile of v2, /device:TPU:1, one launch (start us, length us, event | category | flops | bytes accessed | tf_op | source)
XLA Modules:
  0.0 1107.3 jit_solution(10944119894120984481)
XLA Ops:
  7.3 1.4 convert_reduce_fusion
  8.8 1.6 fusion.2
  20.1 64.8 %all-gather.7.cloned.1.call-done = bf16[4,1024,1024]{2,0,1:T(4,128)(2,1)} async-done(((bf16[4,8,1024]{2,0,1:T(4,128)(2,1)}), bf16[4,1024,1024]{2,0,1:T(4,128)(2,1)}) %all-gather.7.cloned.1.call-update) | async-done | bytes 8388624 | tf_op jit(solution)/shard_map/all_gather | solution.py:366
  85.0 13.7 %copy.125 = bf16[4,1024,1024]{1,2,0:T(8,128)(2,1)} copy(bf16[4,1024,1024]{2,0,1:T(4,128)(2,1)} %all-gather.7.cloned.1.call-done) | data formatting | bytes 16777216 | tf_op jit(solution)/shard_map/all_gather | solution.py:366
  99.7 106.4 %att_safe.6 = (bf16[128,8,512]{2,1,0:T(8,128)(2,1)}, bf16[32,1024]{1,0:T(8,128)(2,1)}) custom-call(bf16[8,64,1024]{2,1,0:T(8,128)(2,1)} %bitcast.206, bf16[4,1024,1024]{2,1,0:T(8,128)(2,1)} %bitcast.205, f32[1024,128]{1,0:T(8,128)} %broadcast_in_dim.12.mask_ref, f32[64,2]{1,0:T(8,128)} %bitcast.219, bf16[256,256]{1,0:T(8,128)(2,1)} %pad.57.wqvt_ref, ...), custom_call_target="tpu_custom_call" | custom-call | tf_op jit(solution)/shard_map/att_safe/pallas_call | solution.py:306
  211.4 1.9 copy.135
  213.3 1.2 copy.136
  214.5 1.6 copy.143.z_ref
  216.1 61.3 %all-gather.9.cloned.1.call-done.bias_ref = bf16[4,1024,1024]{2,1,0:T(8,128)(2,1)} async-done(((bf16[4,8,1024]{2,1,0:T(8,128)(2,1)}), bf16[4,1024,1024]{2,1,0:T(8,128)(2,1)}) %all-gather.9.cloned.1.call-update) | async-done | bytes 8388624 | tf_op jit(solution)/shard_map/all_gather | solution.py:374
  277.4 107.1 %att_safe.7 = (bf16[128,8,512]{2,1,0:T(8,128)(2,1)}, bf16[32,1024]{1,0:T(8,128)(2,1)}) custom-call(bf16[8,64,1024]{2,1,0:T(8,128)(2,1)} %copy.143.z_ref, bf16[4,1024,1024]{2,1,0:T(8,128)(2,1)} %all-gather.9.cloned.1.call-done.bias_ref, f32[1024,128]{1,0:T(8,128)} %broadcast_in_dim.12.mask_ref, f32[64,2]{1,0:T(8,128)} %bitcast.222, ...), custom_call_target="tpu_custom_call" | custom-call | tf_op jit(solution)/shard_map/att_safe/pallas_call | solution.py:306
  389.9 1.9 copy.146
  391.9 1.2 copy.147
  393.0 1.6 copy.154.z_ref
  394.6 60.6 %all-gather.11.cloned.1.call-done.bias_ref = bf16[4,1024,1024]{2,1,0:T(8,128)(2,1)} async-done(((bf16[4,8,1024]{2,1,0:T(8,128)(2,1)}), bf16[4,1024,1024]{2,1,0:T(8,128)(2,1)}) %all-gather.11.cloned.1.call-update) | async-done | bytes 8388624 | tf_op jit(solution)/shard_map/all_gather | solution.py:374
  455.2 107.0 %att_safe.8 = (bf16[128,8,512]{2,1,0:T(8,128)(2,1)}, bf16[32,1024]{1,0:T(8,128)(2,1)}) custom-call(bf16[8,64,1024]{2,1,0:T(8,128)(2,1)} %copy.154.z_ref, bf16[4,1024,1024]{2,1,0:T(8,128)(2,1)} %all-gather.11.cloned.1.call-done.bias_ref, f32[1024,128]{1,0:T(8,128)} %broadcast_in_dim.12.mask_ref, f32[64,2]{1,0:T(8,128)} %bitcast.228, ...), custom_call_target="tpu_custom_call" | custom-call | tf_op jit(solution)/shard_map/att_safe/pallas_call | solution.py:306
  567.5 1.9 copy.157
  569.5 1.2 copy.158
  570.6 1.6 copy.165.z_ref
  572.2 60.8 %all-gather.13.cloned.1.call-done.bias_ref = bf16[4,1024,1024]{2,1,0:T(8,128)(2,1)} async-done(((bf16[4,8,1024]{2,1,0:T(8,128)(2,1)}), bf16[4,1024,1024]{2,1,0:T(8,128)(2,1)}) %all-gather.13.cloned.1.call-update) | async-done | bytes 8388624 | tf_op jit(solution)/shard_map/all_gather | solution.py:374
  633.1 107.0 %att_safe.9 = (bf16[128,8,512]{2,1,0:T(8,128)(2,1)}, bf16[32,1024]{1,0:T(8,128)(2,1)}) custom-call(bf16[8,64,1024]{2,1,0:T(8,128)(2,1)} %copy.165.z_ref, bf16[4,1024,1024]{2,1,0:T(8,128)(2,1)} %all-gather.13.cloned.1.call-done.bias_ref, f32[1024,128]{1,0:T(8,128)} %broadcast_in_dim.12.mask_ref, f32[64,2]{1,0:T(8,128)} %bitcast.230, ...), custom_call_target="tpu_custom_call" | custom-call | tf_op jit(solution)/shard_map/att_safe/pallas_call | solution.py:306
  745.6 1.9 copy.168
  747.5 1.2 copy.169
  748.7 1.6 copy.176.z_ref
  750.3 60.6 %all-gather.15.cloned.1.call-done.bias_ref = bf16[4,1024,1024]{2,1,0:T(8,128)(2,1)} async-done(((bf16[4,8,1024]{2,1,0:T(8,128)(2,1)}), bf16[4,1024,1024]{2,1,0:T(8,128)(2,1)}) %all-gather.15.cloned.1.call-update) | async-done | bytes 8388624 | tf_op jit(solution)/shard_map/all_gather | solution.py:374
  810.9 107.0 %att_safe.10 = (bf16[128,8,512]{2,1,0:T(8,128)(2,1)}, bf16[32,1024]{1,0:T(8,128)(2,1)}) custom-call(bf16[8,64,1024]{2,1,0:T(8,128)(2,1)} %copy.176.z_ref, bf16[4,1024,1024]{2,1,0:T(8,128)(2,1)} %all-gather.15.cloned.1.call-done.bias_ref, f32[1024,128]{1,0:T(8,128)} %broadcast_in_dim.12.mask_ref, f32[64,2]{1,0:T(8,128)} %bitcast.226, ...), custom_call_target="tpu_custom_call" | custom-call | tf_op jit(solution)/shard_map/att_safe/pallas_call | solution.py:306
  922.4 1.9 copy.179
  924.4 1.2 copy.180
  925.6 1.6 copy.186.z_ref
  927.2 61.5 %all-gather.17.cloned.1.call-done.bias_ref = bf16[4,1024,1024]{2,1,0:T(8,128)(2,1)} async-done(((bf16[4,8,1024]{2,1,0:T(8,128)(2,1)}), bf16[4,1024,1024]{2,1,0:T(8,128)(2,1)}) %all-gather.17.cloned.1.call-update) | async-done | bytes 8388624 | tf_op jit(solution)/shard_map/all_gather | solution.py:374
  988.7 107.0 %att_safe.11 = (bf16[128,8,512]{2,1,0:T(8,128)(2,1)}, bf16[32,1024]{1,0:T(8,128)(2,1)}) custom-call(bf16[8,64,1024]{2,1,0:T(8,128)(2,1)} %copy.186.z_ref, bf16[4,1024,1024]{2,1,0:T(8,128)(2,1)} %all-gather.17.cloned.1.call-done.bias_ref, f32[1024,128]{1,0:T(8,128)} %broadcast_in_dim.12.mask_ref, f32[64,2]{1,0:T(8,128)} %bitcast.224, ...), custom_call_target="tpu_custom_call" | custom-call | tf_op jit(solution)/shard_map/att_safe/pallas_call | solution.py:306
  1095.7 1.9 copy.189
  1098.8 1.6 copy.191
  (155 shorter events, 38.3 us)
Async XLA Ops:
  6.5 3.9 copy-start
  6.5 3.9 copy-start.6
  6.5 78.4 %all-gather.7.cloned.1.call-start = ((), (), s32[]{:S(2)}) async-start(), calls=%async_computation | async-start | bytes 8454144 | tf_op jit(solution)/shard_map/all_gather | solution.py:366
  8.7 3.0 copy-start.9
  8.8 4.3 copy-start.1
  10.4 4.3 copy-start.7
  10.4 5.5 copy-start.2
  10.5 6.8 copy-start.8
  10.5 9.7 copy-start.13
  11.7 265.7 %all-gather.9.cloned.1.call-start = ((), (), s32[]{:S(2)}) async-start(), calls=%async_computation.1 | async-start | bytes 8454144 | tf_op jit(solution)/shard_map/all_gather | solution.py:374
  206.1 249.1 %all-gather.11.cloned.1.call-start = ((), (), s32[]{:S(2)}) async-start(), calls=%async_computation.2 | async-start | bytes 8454144 | tf_op jit(solution)/shard_map/all_gather | solution.py:374
  277.4 109.0 %copy-start.20 = (f32[64,1]{0,1:T(1,128)S(1)}, f32[64,1]{0,1:T(1,128)}, u32[]{:S(2)}) copy-start(f32[64,1]{0,1:T(1,128)} %get-tuple-element.79) | copy-start | bytes 772
  277.4 109.7 %copy-start.5 = (bf16[1,1,64,64]{3,2,1,0:T(8,128)(2,1)S(1)}, bf16[1,1,64,64]{3,2,1,0:T(8,128)(2,1)}, u32[]{:S(2)}) copy-start(bf16[1,1,64,64]{3,2,1,0:T(8,128)(2,1)} %get-tuple-element.36) | copy-start | bytes 24580
  277.4 110.4 %copy-start.21 = (f32[64,1]{0,1:T(1,128)S(1)}, f32[64,1]{0,1:T(1,128)}, u32[]{:S(2)}) copy-start(f32[64,1]{0,1:T(1,128)} %get-tuple-element.73) | copy-start | bytes 772
  277.4 111.1 %copy-start.12 = (f32[2,64]{1,0:T(2,128)S(1)}, f32[2,64]{1,0:T(2,128)}, u32[]{:S(2)}) copy-start(f32[2,64]{1,0:T(2,128)} %get-tuple-element.58) | copy-start | bytes 1540
  384.5 248.6 %all-gather.13.cloned.1.call-start = ((), (), s32[]{:S(2)}) async-start(), calls=%async_computation.3 | async-start | bytes 8454144 | tf_op jit(solution)/shard_map/all_gather | solution.py:374
  455.2 108.7 %copy-start.18 = (f32[64,1]{0,1:T(1,128)S(1)}, f32[64,1]{0,1:T(1,128)}, u32[]{:S(2)}) copy-start(f32[64,1]{0,1:T(1,128)} %get-tuple-element.78) | copy-start | bytes 772
  455.2 109.4 %copy-start.4 = (bf16[1,1,64,64]{3,2,1,0:T(8,128)(2,1)S(1)}, bf16[1,1,64,64]{3,2,1,0:T(8,128)(2,1)}, u32[]{:S(2)}) copy-start(bf16[1,1,64,64]{3,2,1,0:T(8,128)(2,1)} %get-tuple-element.35) | copy-start | bytes 24580
  455.2 110.2 %copy-start.19 = (f32[64,1]{0,1:T(1,128)S(1)}, f32[64,1]{0,1:T(1,128)}, u32[]{:S(2)}) copy-start(f32[64,1]{0,1:T(1,128)} %get-tuple-element.72) | copy-start | bytes 772
  455.2 110.9 %copy-start.11 = (f32[2,64]{1,0:T(2,128)S(1)}, f32[2,64]{1,0:T(2,128)}, u32[]{:S(2)}) copy-start(f32[2,64]{1,0:T(2,128)} %get-tuple-element.62) | copy-start | bytes 1540
  562.3 248.6 %all-gather.15.cloned.1.call-start = ((), (), s32[]{:S(2)}) async-start(), calls=%async_computation.4 | async-start | bytes 8454144 | tf_op jit(solution)/shard_map/all_gather | solution.py:374
  633.1 109.0 %copy-start.16 = (f32[64,1]{0,1:T(1,128)S(1)}, f32[64,1]{0,1:T(1,128)}, u32[]{:S(2)}) copy-start(f32[64,1]{0,1:T(1,128)} %get-tuple-element.82) | copy-start | bytes 772
  633.1 109.7 %copy-start.3 = (bf16[1,1,64,64]{3,2,1,0:T(8,128)(2,1)S(1)}, bf16[1,1,64,64]{3,2,1,0:T(8,128)(2,1)}, u32[]{:S(2)}) copy-start(bf16[1,1,64,64]{3,2,1,0:T(8,128)(2,1)} %get-tuple-element.34) | copy-start | bytes 24580
  633.1 110.4 %copy-start.17 = (f32[64,1]{0,1:T(1,128)S(1)}, f32[64,1]{0,1:T(1,128)}, u32[]{:S(2)}) copy-start(f32[64,1]{0,1:T(1,128)} %get-tuple-element.76) | copy-start | bytes 772
  633.1 111.1 %copy-start.10 = (f32[2,64]{1,0:T(2,128)S(1)}, f32[2,64]{1,0:T(2,128)}, u32[]{:S(2)}) copy-start(f32[2,64]{1,0:T(2,128)} %get-tuple-element.57) | copy-start | bytes 1540
  740.1 248.6 %all-gather.17.cloned.1.call-start = ((), (), s32[]{:S(2)}) async-start(), calls=%async_computation.5 | async-start | bytes 8454144 | tf_op jit(solution)/shard_map/all_gather | solution.py:374
  810.9 108.7 %copy-start.14 = (f32[64,1]{0,1:T(1,128)S(1)}, f32[64,1]{0,1:T(1,128)}, u32[]{:S(2)}) copy-start(f32[64,1]{0,1:T(1,128)} %get-tuple-element.77) | copy-start | bytes 772
  810.9 110.1 %copy-start.15 = (f32[64,1]{0,1:T(1,128)S(1)}, f32[64,1]{0,1:T(1,128)}, u32[]{:S(2)}) copy-start(f32[64,1]{0,1:T(1,128)} %get-tuple-element.71) | copy-start | bytes 772
Sparse Core Ops, SparseCore 0:
  11.8 73.1 all-gather.6
  206.2 71.0 all-gather.8
  384.6 70.5 all-gather.10
  562.4 70.5 all-gather.12
  740.2 70.5 all-gather.14
  918.1 70.5 all-gather.16

commit v3 on v0

v3 whole, which is shorter than its diff:
```python
import functools
import jax
import jax.numpy as jnp
from jax import lax
from jax.experimental import pallas as pl
from jax.experimental.pallas import tpu as pltpu
from jax.sharding import PartitionSpec as P

F32 = jnp.float32
BF16 = jnp.bfloat16
EPS = 1e-5
NEG = -1e9
LOG2E = 1.4426950408889634
TZ, TY, TX, TC = 4, 4, 4, 2
PARTS = (((2, 1, 0), 0, 3), ((1, 0, 2), 3, 3), ((0, 2, 1), 6, 2))
MESH = pl.DeviceIdType.MESH


def _ln_t(x, gamma, beta):
    mu = jnp.mean(x, axis=0, keepdims=True)
    d = x - mu
    var = jnp.mean(d*d, axis=0, keepdims=True)
    return (d * lax.rsqrt(var + EPS) * gamma + beta).astype(BF16)


def mega_kernel(R, N, C, H, LAG, ME,
                z_ref, mask_ref, lnw_ref, wqvt_ref, wk2_ref, bg_ref, wo_ref, bo_ref, wbn_ref,
                out_ref,
                k_s, q_s, v_s, g_s, z_s, o_s, y_s, zt_s, bias_s, x_s, r_s, G,
                a2a_send, a2a_recv, own_sem, ag_send, ag_recv):
    ps, jb = pl.program_id(0), pl.program_id(1)
    n_pass, n_blk = lnw_ref.shape[0], 4
    others = pl.ds(0, TZ*TY*TX*TC-1)
    me = lax.axis_index('dap')
    n_dev = TZ*TY*TX*TC
    D = C // H
    QB = N // 4
    KC = 128
    CH = N // KC
    DB = QB // R
    par, nxt = lax.rem(ps, 2), lax.rem(ps + 1, 2)
    q0 = pl.multiple_of(jb * QB, QB)
    core = lax.rem(me, TC)
    at = (lax.div(me, TY*TX*TC), lax.rem(lax.div(me, TX*TC), TY), lax.rem(lax.div(me, TC), TX))

    def dev(z, y, x, c):
        return {'dap': ((z*TY + y)*TX + x)*TC + c}

    def moved(axis, by):
        p = list(at)
        p[axis] = lax.rem(p[axis] + by, 4)
        return p

    def chunk(g, b, sel, u0, nu):
        return G.at[g, b, sel[0], sel[1], sel[2], core, pl.ds(u0, nu)]

    def copy(g, b, k, sel, u0, nu, to, c):
        r = chunk(g, b, sel, u0, nu)
        return pltpu.make_async_remote_copy(r, r, ag_send.at[g, b, k], ag_recv.at[g, b, k],
                                            device_id=dev(*to, c), device_id_type=MESH)

    def landed(g, b, k, sem):
        sel = ((0, 0, pl.ds(0, 3)), (0, pl.ds(0, 3), slice(None)), (pl.ds(0, 2), slice(None), slice(None)),
               (0, slice(None), slice(None)), (slice(None),)*3)[k]
        r = G.at[g, b, sel[0], sel[1], sel[2], 0]
        pltpu.make_async_copy(r, r, sem.at[g, b, k]).wait()

    def stage(k, g, b):
        if k > 0:
            landed(g, b, k-1, ag_recv)
        if k == 5:
            for j in range(5):
                landed(g, b, j, ag_send)
            return
        if k == 4:
            r = G.at[g, b, :, :, :, core]
            pltpu.make_async_remote_copy(r, r, ag_send.at[g, b, 4], ag_recv.at[g, b, 4],
                                         device_id=dev(*at, 1-core), device_id_type=MESH).start()
            return
        for (a0, a1, a2), u0, nu in PARTS:
            sel = list(at)
            if k == 0:
                for by in (1, 3, 2):
                    copy(g, b, k, sel, u0, nu, moved(a0, by), core).start()
            elif k == 1:
                sel[a0] = slice(None)
                for by in (1, 3, 2):
                    copy(g, b, k, sel, u0, nu, moved(a1, by), core).start()
            elif k == 2:
                sel[a0] = sel[a1] = slice(None)
                for by in (1, 3):
                    copy(g, b, k, sel, u0, nu, moved(a2, by), core).start()
            else:
                for by, half in ((1, 0), (3, 2)):
                    sel[a0] = slice(None)
                    sel[a1] = pl.ds(half, 2)
                    sel[a2] = lax.rem(at[a2] + 4 - by, 4)
                    copy(g, b, k, sel, u0, nu, moved(a2, by), core).start()

    def slot(s, p, lo, hi):
        for k in range(6):
            b = s - k
            if hi - k >= 0 and lo - k < n_blk:
                @pl.when((b >= 0) & (b < n_blk) & (p < n_pass-1))
                def _():
                    stage(k, lax.rem(p + 1, 2), b)
            if lo - k + 6 < 4:
                @pl.when((b < 0) & (b + 6 < n_blk) & (p >= 1))
                def _():
                    stage(k, lax.rem(p, 2), b + 6)

    def put_bias(g, b, rows):
        for h in range(H):
            for t in range(2):
                G[g, b, at[0], at[1], at[2], core, 2*h+t] = rows[h*R:(h+1)*R, t*128:(t+1)*128]

    def bias_rows(p, y):
        return jnp.dot(wbn_ref[p], y, preferred_element_type=F32).astype(BF16)

    def prep(i, _):
        y = _ln_t(z_s[i].astype(F32), lnw_ref[ps, :, 0:1], lnw_ref[ps, :, 1:2])
        p = jnp.dot(wqvt_ref[ps], y, preferred_element_type=F32)
        k_s[i] = jnp.dot(y.T, wk2_ref[ps], preferred_element_type=F32).astype(BF16)
        q = p[0:C].astype(BF16).astype(F32) * (LOG2E * D ** -0.5)
        qh = q.astype(BF16)
        ql = (q - qh.astype(F32)).astype(BF16)
        for h in range(H):
            q_s[i, 2*D*h:2*D*h+D] = qh[D*h:D*h+D]
            q_s[i, 2*D*h+D:2*D*h+2*D] = ql[D*h:D*h+D]
        v_s[i] = p[C:2*C].astype(BF16)
        g_s[i] = jax.nn.sigmoid(p[2*C:3*C] + bg_ref[ps])
        return 0

    def unpack(w, _):
        t = r_s[par, pl.ds(w*16, 16)].reshape(128, R*C).astype(F32).T
        x = [t[i*C:(i+1)*C] for i in range(R)]
        lane = lax.broadcasted_iota(jnp.int32, (C, 128), 1)
        for bit in (1, 2, 4):
            odd = (lane & bit) != 0
            for i in range(R):
                if not i & bit:
                    a, b = x[i], x[i | bit]
                    x[i] = jnp.where(odd, pltpu.roll(b, bit, 1), a)
                    x[i | bit] = jnp.where(odd, b, pltpu.roll(a, 128-bit, 1))
        for i in range(R):
            z_s[i, :, pl.ds(pl.multiple_of(w*128, 128), 128)] = x[i].astype(BF16)
        return 0

    @pl.when((jb == 0) & (ps == 0))
    def _():
        barrier = pltpu.get_barrier_semaphore()
        def greet(k, _):
            pl.semaphore_signal(barrier, inc=1, device_id={'dap': lax.rem(me + k, n_dev)}, device_id_type=MESH)
            return 0
        lax.fori_loop(1, n_dev, greet, 0)
        def first(b, _):
            qs = pl.ds(pl.multiple_of(b*QB, QB), QB)
            for i in range(R):
                zb = z_ref[i, :, qs]
                z_s[i, :, qs] = zb
                y_s[i*C:(i+1)*C] = _ln_t(zb.astype(F32), lnw_ref[0, :, 0:1], lnw_ref[0, :, 1:2])
            put_bias(0, b, bias_rows(0, y_s[...]))
            return 0
        lax.fori_loop(0, n_blk, first, 0)
        pl.semaphore_wait(barrier, n_dev - 1)
        def gather(k):
            def each(b, _):
                stage(k, 0, b)
                return 0
            lax.fori_loop(0, n_blk, each, 0)
        gather(0)
        lax.fori_loop(0, R//2, prep, 0)
        gather(1)
        lax.fori_loop(R//2, R, prep, 0)
        for k in range(2, 6):
            gather(k)

    @pl.when((jb == 0) & (ps > 0))
    def _():
        pltpu.make_async_copy(r_s.at[par, others], r_s.at[par, others], a2a_recv.at[par]).wait()
        pltpu.make_async_copy(r_s.at[par, others], r_s.at[par, others], a2a_send).wait()
        lax.fori_loop(0, N//128, unpack, 0)
        lax.fori_loop(0, R//2, prep, 0)
        slot(4, ps-1, 4, 4)
        lax.fori_loop(R//2, R, prep, 0)
        slot(5, ps-1, 5, 5)

    @pl.when(ps == 0)
    def _():
        def each(h, _):
            for b in range(n_blk):
                for t in range(2):
                    v = G[0, b, jb, :, :, :, 2*h+t].reshape(QB, 128).astype(F32).T
                    rows = slice((2*b+t)*128, (2*b+t+1)*128)
                    for w in range(2):
                        bias_s[h, rows, w*128:(w+1)*128] = v[:, w*128:(w+1)*128] * LOG2E + mask_ref[rows]
            return 0
        lax.fori_loop(0, H, each, 0)

    @pl.when(ps > 0)
    def _():
        def each(h, _):
            for m in range(CH):
                for w in range(2):
                    v = G[par, jb, m//2, 2*(m % 2):2*(m % 2)+2, :, :, 2*h+w].reshape(128, 128).astype(F32)
                    bias_s[h, m*128:(m+1)*128, w*128:(w+1)*128] = v * LOG2E + mask_ref[m*128:(m+1)*128]
            return 0
        lax.fori_loop(0, H, each, 0)

    zl = jnp.zeros((KC, 256-2*C), BF16)
    zp = jnp.zeros((KC, QB), BF16)
    zv = jnp.zeros((2*D, 256-KC), BF16)
    zq = jnp.zeros((2*D, QB), BF16)
    ones = jnp.where(lax.broadcasted_iota(jnp.int32, (D, KC), 0) == 0, 1.0, 0.0).astype(BF16)
    steps = [(h, t, c) for h in range(H) for t in range(R//ME) for c in range(CH)]
    S = len(steps)
    es, ss, acc = {}, {}, [None]*ME
    for n in range(-LAG, S):
        if n >= 0:
            h, t, c = steps[n]
            b = bias_s[h, c*KC:(c+1)*KC]
            for m in range(ME):
                es[m] = jnp.exp2(ss.pop((n, m)) + b).astype(BF16)
        for m in range(ME):
            rows = []
            w = zp
            if n+LAG < S:
                h2, t2, c2 = steps[n+LAG]
                i2 = ME*t2+m
                w = jnp.concatenate([zq]*h2 + [q_s[i2, 2*D*h2:2*D*(h2+1), pl.ds(q0, QB)]] + [zq]*(H-1-h2), axis=0)
                rows.append(jnp.concatenate([zl, k_s[i2, c2*KC:(c2+1)*KC]], axis=1))
            if n >= 0:
                vv = jnp.concatenate([v_s[ME*t+m, D*h:D*h+D, c*KC:(c+1)*KC], ones], axis=0)
                rows.append(jnp.concatenate([vv, zv], axis=1))
            o = jnp.dot(jnp.concatenate(rows, axis=0), jnp.concatenate([es.pop(m) if n >= 0 else zp, w], axis=0),
                        preferred_element_type=F32)
            if n+LAG < S:
                ss[n+LAG, m] = o[0:KC]
            if n >= 0:
                i = ME*t+m
                o = o[-2*D:]
                acc[m] = o if c == 0 else acc[m] + o
                if c == CH-1:
                    a = acc[m][0:D] / acc[m][D:D+1]
                    o_s[i, D*h:D*h+D] = (g_s[i, D*h:D*h+D, pl.ds(q0, QB)] * a).astype(BF16)

    pn = lax.rem(ps + 1, n_pass)

    def upd(i, _):
        u = jnp.dot(wo_ref[ps], o_s[i], preferred_element_type=F32) + bo_ref[ps]
        zn = (z_s[i, :, pl.ds(q0, QB)].astype(F32) + u).astype(BF16)
        rows = pl.ds(pl.multiple_of(i*C, C), C)
        zt_s[rows] = zn
        y_s[rows] = _ln_t(zn.astype(F32), lnw_ref[pn, :, 0:1], lnw_ref[pn, :, 1:2])
        return 0
    lax.fori_loop(0, R, upd, 0)
    x_s[pl.ds(jb*DB, DB)] = zt_s[...].T.reshape(DB, R, R*C)

    @pl.when(ps < n_pass-1)
    def _():
        put_bias(nxt, jb, bias_rows(pn, y_s[...]))

    def send(k, _):
        d = jb*DB + k
        @pl.when(d != me)
        def _():
            pltpu.make_async_remote_copy(x_s.at[d], r_s.at[nxt, me], a2a_send, a2a_recv.at[nxt],
                                         device_id={'dap': d}, device_id_type=MESH).start()
        return 0
    lax.fori_loop(0, DB, send, 0)

    @pl.when((me >= jb*DB) & (me < (jb+1)*DB))
    def _():
        r_s[nxt, me] = x_s[me]
    slot(jb, ps, 0, 3)

    @pl.when((ps == n_pass-1) & (jb == n_blk-1))
    def _():
        pltpu.make_async_copy(r_s.at[nxt, others], r_s.at[nxt, others], a2a_recv.at[nxt]).wait()
        pltpu.make_async_copy(r_s.at[nxt, others], r_s.at[nxt, others], a2a_send).wait()
        out = pltpu.make_async_copy(r_s.at[nxt], out_ref, own_sem)
        out.start()
        out.wait()


def mega(z, mask, lnw, wqvt, wk2, bg, wo, bo, wbn, LAG=2, ME=4):
    R, C, N = z.shape
    n_pass = lnw.shape[0]
    H = wbn.shape[1] // R
    QB = N // 4
    full = lambda a: pl.BlockSpec(a.shape, lambda p, j: (0,)*a.ndim, pipeline_mode=pl.Buffered(1))
    args = (z, mask, lnw, wqvt, wk2, bg, wo, bo, wbn)
    flops = n_pass * (4*R*H*N*N*(C//H) + 2*R*N*C*6*C)
    return pl.pallas_call(
        functools.partial(mega_kernel, R, N, C, H, LAG, ME),
        grid=(n_pass, 4),
        in_specs=[full(a) for a in args],
        out_specs=pl.BlockSpec(memory_space=pl.ANY),
        out_shape=jax.ShapeDtypeStruct((N//R, R, R*C), BF16),
        scratch_shapes=[pltpu.VMEM((R, N, 2*C), BF16), pltpu.VMEM((R, 2*C, N), BF16), pltpu.VMEM((R, C, N), BF16),
                        pltpu.VMEM((R, C, N), F32), pltpu.VMEM((R, C, N), BF16), pltpu.VMEM((R, C, QB), BF16),
                        pltpu.VMEM((R*C, QB), BF16), pltpu.VMEM((R*C, QB), BF16), pltpu.VMEM((H, N, QB), F32),
                        pltpu.VMEM((N//R, R, R*C), BF16), pltpu.VMEM((2, N//R, R, R*C), BF16),
                        pltpu.VMEM((2, 4, TZ, TY, TX, TC, 2*H, R, 128), BF16),
                        pltpu.SemaphoreType.DMA, pltpu.SemaphoreType.DMA((2,)), pltpu.SemaphoreType.DMA,
                        pltpu.SemaphoreType.DMA((2, 4, 5)), pltpu.SemaphoreType.DMA((2, 4, 5))],
        compiler_params=pltpu.CompilerParams(dimension_semantics=("arbitrary", "arbitrary"), vmem_limit_bytes=60*2**20,
                                             collective_id=0, has_side_effects=True),
        cost_estimate=pl.CostEstimate(flops=flops, bytes_accessed=4*2**20, transcendentals=n_pass*R*H*N*N),
        name="mega",
    )(*args)


def prep_weights(ln_w, w_in, b_g, w_b, w_o, b_o, R):
    n, C, H = w_b.shape
    D = C // H
    lnw = jnp.swapaxes(ln_w.astype(F32), 1, 2)
    wt = jnp.swapaxes(w_in, 1, 2)
    wqvt = jnp.concatenate([wt[:, 0:C], wt[:, 2*C:4*C]], axis=1)
    wk = w_in[:, :, C:2*C].reshape(n, C, H, 1, D)
    wk2 = jnp.broadcast_to(wk, (n, C, H, 2, D)).reshape(n, C, 2*C)
    eye = jnp.eye(R, dtype=w_b.dtype)
    wbn = (jnp.swapaxes(w_b, 1, 2)[:, :, None, None, :] * eye[None, None, :, :, None]).reshape(n, H*R, R*C)
    col = lambda a: a.astype(F32)[:, :, None]
    return lnw, wqvt, wk2, col(b_g), jnp.swapaxes(w_o, 1, 2), col(b_o), wbn


def _ln_rows(x, w):
    x = x.astype(F32)
    mu = jnp.mean(x, axis=-1, keepdims=True)
    var = jnp.mean(jnp.square(x - mu), axis=-1, keepdims=True)
    y = (x - mu) * lax.rsqrt(var + EPS)
    return (y * w[0].astype(F32) + w[1].astype(F32)).astype(BF16)


def _rows(zl, bias, lw, wi, bg, wo, bo):
    h, n, _ = bias.shape
    c = zl.shape[-1]
    d = c // h

    def row(zr):
        y = _ln_rows(zr, lw)
        proj = jnp.transpose(jnp.dot(y, wi, preferred_element_type=F32).reshape(n, 4, h, d), (1, 2, 0, 3))
        gate = jax.nn.sigmoid(proj[3] + bg.astype(F32).reshape(h, 1, d))

        def head(a):
            q, k, v, b = a
            s = jnp.dot(q, k.T, preferred_element_type=F32) * d ** -0.5 + b
            return jnp.dot(jax.nn.softmax(s, axis=-1).astype(BF16), v, preferred_element_type=F32)

        o = lax.map(head, (*(a.astype(BF16) for a in proj[:3]), bias))
        o = jnp.transpose((gate * o).astype(BF16), (1, 0, 2)).reshape(n, c)
        return (zr.astype(F32) + jnp.dot(o, wo, preferred_element_type=F32) + bo.astype(F32)).astype(BF16)

    return lax.map(row, zl)


def _safe_to_skip_max(ws):
    ln_w, w_in, b_g, w_b, w_o, b_o = (a.astype(F32) for a in ws)
    n, C, H = w_b.shape
    D = C // H
    g, b = ln_w[:, 0], ln_w[:, 1]
    w = w_in.reshape(n, C, 4, H, D)[:, :, 0:3]
    wg = w * g[:, :, None, None, None]
    gram = jnp.sum(wg[..., :, None] * wg[..., None, :], axis=1)
    top = lambda m: jnp.sqrt(jnp.max(jnp.sum(jnp.abs(m), axis=-1), axis=-1) * C)
    both = top(jnp.sum(gram[:, 0, :, :, :, None] * gram[:, 1, :, None, :, :], axis=-2)) * C ** 0.5
    one = top(gram)
    off = jnp.sqrt(jnp.sum(jnp.square(jnp.sum(w * b[:, :, None, None, None], axis=1)), axis=-1))
    q, k, v = (one[:, a] + off[:, a] for a in range(3))
    qk = both + q * k - one[:, 0] * one[:, 1] + 0.02 * q * k
    nb = jnp.sqrt(jnp.sum(jnp.square(w_b * g[..., None]), axis=1) * C) + jnp.abs(jnp.sum(w_b * b[..., None], axis=1))
    return jnp.all((LOG2E * (qk * D ** -0.5 + 1.02 * nb) <= 100.0) & (v <= 2.0 ** 14))


def solution(mesh):
    def local(zl, res_mask, ln_w, w_in, b_g, w_b, w_o, b_o):
        R, N, C = zl.shape
        G = N // R
        mask_bias = jnp.where(res_mask > 0, 0.0, NEG).astype(F32)
        n = ln_w.shape[0] * ln_w.shape[1]
        ws = tuple(a.reshape(n, *a.shape[2:]) for a in (ln_w, w_in, b_g, w_b, w_o, b_o))

        def fast(zl):
            mask = jnp.broadcast_to(mask_bias[:, None], (N, 128))
            x = mega(jnp.swapaxes(zl, 1, 2), mask, *prep_weights(*ws, R))
            return jnp.transpose(x.reshape(G, R, R, C), (1, 0, 2, 3)).reshape(R, N, C)

        def exact(zl):
            def one(p, z):
                lw, wi, bg, wb, wo, bo = (lax.dynamic_index_in_dim(a, p, keepdims=False) for a in ws)
                b = jnp.dot(_ln_rows(z, lw).reshape(R*N, C), wb, preferred_element_type=F32).astype(BF16)
                b = lax.all_gather(b.reshape(R, N, -1), 'dap', axis=0, tiled=True)
                z = _rows(z, jnp.transpose(b, (2, 0, 1)).astype(F32) + mask_bias, lw, wi, bg, wo, bo)
                return jnp.swapaxes(lax.all_to_all(z, 'dap', 1, 0, tiled=True), 0, 1)
            return lax.fori_loop(0, n, one, zl)

        return lax.cond(_safe_to_skip_max(ws), fast, exact, zl)

    rows = P(('data', 'dap'))
    return jax.shard_map(local, mesh=mesh,
                         in_specs=(rows, P('data'), P(), P(), P(), P(), P(), P()),
                         out_specs=rows, check_vma=False)
```

time: 1550 us -> 390 us (0.25); the launches traced: 1530 us -> 390 us
  matrix products: 649 us -> 0 us
  Pallas kernels: 0 us -> 354 us
  waiting for transfers between devices: 353 us -> 0 us
  local copies, waits for them, and re-layouts: 229 us -> 12.2 us
  blocking collectives: 148 us -> 0 us
  other arithmetic: 140 us -> 9.04 us
    pallas_call x0 -> x1, Pallas kernels: none -> 354 us  [mega(): pl.pallas_call(functools.partial(mega_kernel, R, N, C, H, LAG, ME), grid=...]
    all_gather x6 -> x0, waiting for transfers between devices: 353 us -> none  [_tri_start(): b = lax.all_gather(b.reshape(r, n, -1), 'dap', axis=0, tiled=True)]
    sub x6 -> x0, matrix products: 342 us -> none  [block(): p = jax.nn.softmax(s, axis=-1).astype(BF16)]
    dot_general x24 -> x0, matrix products: 307 us -> none  [the longest x6 254 us: block(): o = jnp.einsum('bhjk,bkhd->bjhd', p, v, preferred_element_type=F32)]
    all_to_all x6 -> x0, blocking collectives: 148 us -> none  [the longest x3 74 us: local(): zt = lax.all_to_all(zl, 'dap', 1, 0, tiled=True)]
    add x6 -> x2, local copies, waits for them, and re-layouts: 115 us -> 0.19 us  [_safe_to_skip_max(): q, k, v = (one[:, a] + off[:, a] for a in range(3))]
    add x6 -> x1, other arithmetic: 60.4 us -> 0.01 us  [_safe_to_skip_max(): q, k, v = (one[:, a] + off[:, a] for a in range(3))]
    convert_element_type x28 -> x0, local copies, waits for them, and re-layouts: 46.6 us -> none  [the longest x11 34.3 us: block(): return (zb.astype(F32) + upd.reshape(rb, n, c)).astype(BF16)]
  transfers between devices with their start and end apart: 6 -> 0, of which waited for: 6 -> 0; matrix products, arithmetic and copies ran while one was open for 3% -> 0% of each run, Pallas kernels for 0% -> 0%
where the time goes in v3:
time: 390 us
  Pallas kernels  354 us (91%)
  between operations  14.2 us (4%)
  local copies, waits for them, and re-layouts  12.2 us (3%)
  other arithmetic  9.04 us (2%)
    pallas_call x1, Pallas kernels, mega(): pl.pallas_call(functools.partial(mega_kernel, R, N, C, H, LAG, ME), grid=...  354 us

profile of v3, /device:TPU:1, one launch (start us, length us, event | category | flops | bytes accessed | tf_op | source)
XLA Modules:
  0.0 390.0 jit_solution(2400904316097989556)
XLA Ops:
  6.6 0.8 bitcast_convert_fusion.6
  7.4 1.2 copy.133
  8.5 0.3 convert_multiply_fusion.1
  8.8 2.5 multiply_reduce_fusion
  11.3 0.3 abs_reduce_fusion
  11.6 0.1 reduce_max.28
  11.7 0.1 copy.134
  11.8 0.1 multiply_reduce_fusion.2
  11.9 0.1 copy.135
  12.3 1.1 multiply_reduce_fusion.1
  13.5 0.1 abs_reduce_fusion.1
  13.7 0.1 copy.141
  14.0 0.7 and_reduce_fusion
  15.3 0.7 copy.143
  16.0 0.6 reshape.210
  16.7 365.5 %conditional.1 = (bf16[8,1024,64]{1,2,0:T(8,128)(2,1)S(1)}) conditional(s32[]{:T(128)} %convert_element_type.134, (bf16[6,2,64]{2,1,0:T(2,128)(2,1)}, bf16[6,64,256]{1,2,0:T(8,128)(2,1)S(1)}, bf16[6,64]{1,0:T(8,128)(2,1)S(1)}, bf16[6,64,4]{1,2,0:T(4,128)(2,1)S(1)}, f32[1024]{0:T(1024)S(1)}, /*index=5*/bf16[6,64,64]{1,2,0:T(8,128)(2,1)}, ...), branch_computations={%region_11.24_spmd, %region_24.25_spmd} | conditional | flops 15301216256 | bytes 134329024 | solution.py:398
  16.7 0.8 pad_maximum_fusion.wqvt_ref
  17.5 0.8 copy.128.wk2_ref
  18.3 0.7 bitcast_convert_fusion.4
  19.0 0.8 copy.129.bg_ref
  19.8 0.8 copy.130.bo_ref
  20.7 0.3 mul.168
  21.0 0.1 mul.170
  21.2 0.7 broadcast_multiply_fusion.2.wbn_ref
  21.8 1.0 broadcast_in_dim.43.mask_ref
  22.8 0.1 copy.146
  23.0 0.7 convert_bitcast_fusion.1.lnw_ref
  23.7 354.5 %mega.1 = bf16[128,8,512]{2,1,0:T(8,128)(2,1)} custom-call(bf16[8,64,1024]{2,1,0:T(8,128)(2,1)S(1)} %bitcast.239, f32[1024,128]{1,0:T(8,128)} %broadcast_in_dim.43.mask_ref, f32[6,64,2]{2,1,0:T(8,128)} %convert_bitcast_fusion.1.lnw_ref, bf16[6,192,64]{2,1,0:T(8,128)(2,1)} %pad_maximum_fusion.wqvt_ref, bf16[6,64,128]{2,1,0:T(8,128)(2,1)} %copy.128.wk2_ref, ...), custom_call_target="tpu_custom_call" | custom-call | flops 15300820992 | bytes 4194304 | tf_op jit(solution)/shard_map/cond/branch_1_fun/mega/pallas_call | solution.py:294
  378.2 1.9 copy.131
  380.1 1.2 copy.132
  381.3 0.8 copy.151
  382.2 1.0 copy-done.3
  (40 shorter events, 0.8 us)
Async XLA Ops:
  6.5 7.3 %copy-start.8 = (bf16[3,2,64,4]{2,3,1,0:T(4,128)(2,1)S(1)}, bf16[3,2,64,4]{2,3,1,0:T(4,128)(2,1)}, u32[]{:S(2)}) copy-start(bf16[3,2,64,4]{2,3,1,0:T(4,128)(2,1)} %param.21) | copy-start | bytes 9220
  6.5 8.7 %copy-start.7 = (bf16[3,2,64,64]{3,2,1,0:T(8,128)(2,1)S(1)}, bf16[3,2,64,64]{3,2,1,0:T(8,128)(2,1)}, u32[]{:S(2)}) copy-start(bf16[3,2,64,64]{3,2,1,0:T(8,128)(2,1)} %param.22) | copy-start | bytes 147460
  6.5 9.5 %copy-start.14 = (s32[1024]{0:T(1024)S(1)}, s32[1024]{0:T(1024)}, u32[]{:S(2)}) copy-start(s32[1024]{0:T(1024)} %param.17) | copy-start | bytes 12292
  6.5 9.5 %copy-start.15 = (bf16[3,2,64]{2,1,0:T(2,128)(2,1)S(1)}, bf16[3,2,64]{2,1,0:T(2,128)(2,1)}, u32[]{:S(2)}) copy-start(bf16[3,2,64]{2,1,0:T(2,128)(2,1)} %param.20) | copy-start | bytes 2308
  6.5 9.5 %copy-start.16 = (bf16[3,2,64]{2,1,0:T(2,128)(2,1)S(1)}, bf16[3,2,64]{2,1,0:T(2,128)(2,1)}, u32[]{:S(2)}) copy-start(bf16[3,2,64]{2,1,0:T(2,128)(2,1)} %param.23) | copy-start | bytes 2308
  6.5 10.1 %copy-start.2 = (bf16[8,1024,64]{1,2,0:T(8,128)(2,1)S(1)}, bf16[8,1024,64]{1,2,0:T(8,128)(2,1)}, u32[]{:S(2)}) copy-start(bf16[8,1024,64]{1,2,0:T(8,128)(2,1)} %param.16) | copy-start | bytes 3145732
  16.7 6.2 %copy-start.13 = (bf16[6,2,64]{2,1,0:T(2,128)(2,1)S(1)}, bf16[6,2,64]{2,1,0:T(2,128)(2,1)}, u32[]{:S(2)}) copy-start(bf16[6,2,64]{2,1,0:T(2,128)(2,1)} %get-tuple-element.432) | copy-start | bytes 4612 | tf_op jit(solution)/shard_map/cond
  16.7 7.0 %copy-start.4 = (bf16[6,64,64]{1,2,0:T(8,128)(2,1)S(1)}, bf16[6,64,64]{1,2,0:T(8,128)(2,1)}, u32[]{:S(2)}) copy-start(bf16[6,64,64]{1,2,0:T(8,128)(2,1)} %get-tuple-element.286) | copy-start | bytes 147460 | tf_op jit(solution)/shard_map/cond
  382.2 1.0 copy-start.3

commit v4 on v3

v4 whole, which is shorter than its diff:
```python
import functools
import jax
import jax.numpy as jnp
from jax import lax
from jax.experimental import pallas as pl
from jax.experimental.pallas import tpu as pltpu
from jax.sharding import PartitionSpec as P

F32 = jnp.float32
BF16 = jnp.bfloat16
EPS = 1e-5
NEG = -1e9
LOG2E = 1.4426950408889634
T = 4
BLOCKS = 4
PARTS = (((2, 1, 0), 0, 3), ((1, 0, 2), 3, 3), ((0, 2, 1), 6, 2))
MESH = pl.DeviceIdType.MESH
HIGH = lax.Precision.HIGHEST


def _ln_t(x, gamma, beta):
    mu = jnp.mean(x, axis=0, keepdims=True)
    d = x - mu
    var = jnp.mean(d*d, axis=0, keepdims=True)
    return (d * lax.rsqrt(var + EPS) * gamma + beta).astype(BF16)


def _place(b, r):
    z, y = r // (2*T), (r // 2) % T
    return z, y, (b + 2*T - z - y) % T, r % 2


def _index(z, y, x, c):
    return ((z*T + y)*T + x)*2 + c


def setup_kernel(R, ln_ref, win_ref, bg_ref, wbt_ref, wo_ref, bo_ref, m_ref,
                 cols_ref, wqvt_ref, wk2_ref, wot_ref, wbn_ref, mask_ref, ok_ref):
    n, H, C = wbt_ref.shape
    D = C // H
    iota = lambda shape, axis: lax.broadcasted_iota(jnp.int32, shape, axis)
    head = iota((C, C), 0) // D == iota((C, C), 1) // D
    lane = iota((C, 2*C), 1)
    twice = (iota((C, 2*C), 0) == (lane // (2*D)) * D + lane % D).astype(F32).astype(BF16)
    mine = iota((H, R, R*C), 1) == iota((H, R, R*C), 2) // C
    nt = lambda a, b: lax.dot_general(a, b, (((1,), (1,)), ((), ())), precision=HIGH, preferred_element_type=F32)
    whole = lambda f, a: f(f(a, axis=1, keepdims=True), axis=0, keepdims=True)
    top = lambda m: whole(lambda a, axis, keepdims: jnp.sum(a, axis=1, keepdims=True) if axis else
                          jnp.max(a, axis=0, keepdims=True), jnp.abs(m))
    good = jnp.ones((1, 1), F32)
    for p in range(n):
        ln = ln_ref[p].astype(F32)
        vecs = jnp.concatenate([ln, bg_ref[p:p+1].astype(F32), bo_ref[p:p+1].astype(F32), jnp.zeros((4, C), F32)], axis=0)
        cols_ref[p] = jnp.concatenate([vecs, jnp.zeros((8, C), F32)], axis=1).T[0:C]
        w = win_ref[p].T
        wqvt_ref[p, 0:C] = w[0:C]
        wqvt_ref[p, C:3*C] = w[2*C:4*C]
        wk = lax.dot_general(w[C:2*C], twice, (((0,), (0,)), ((), ())), preferred_element_type=F32)
        wk2_ref[p] = wk.astype(BF16)
        wot_ref[p] = wo_ref[p].T
        wb = wbt_ref[p].astype(F32)
        rep = jnp.concatenate([wb]*R, axis=1)
        wbn_ref[p] = jnp.where(mine, rep[:, None, :], 0.0).reshape(H*R, R*C).astype(BF16)

        w = w.astype(F32)
        wg = w * ln[0:1]
        gram = [jnp.where(head, nt(wg[a*C:(a+1)*C], wg[a*C:(a+1)*C]), 0.0) for a in range(3)]
        both = jnp.sqrt(top(jnp.dot(gram[0], gram[1], precision=HIGH, preferred_element_type=F32))) * C
        one = [jnp.sqrt(top(g) * C) for g in gram]
        off = jnp.square(jnp.sum(w * ln[1:2], axis=1, keepdims=True))
        per = lambda a: functools.reduce(jnp.maximum, [jnp.sum(off[a*C+h*D:a*C+(h+1)*D], axis=0, keepdims=True) for h in range(H)])
        q, k, v = (one[a] + jnp.sqrt(per(a)) for a in range(3))
        qk = both + q*k - one[0]*one[1] + 0.02*q*k
        nb = jnp.sqrt(jnp.sum(jnp.square(wb * ln[0:1]), axis=1, keepdims=True) * C) + jnp.abs(jnp.sum(wb * ln[1:2], axis=1, keepdims=True))
        s = LOG2E * (qk * D ** -0.5 + 1.02 * jnp.max(nb, axis=0, keepdims=True))
        good = jnp.where((s <= 100.0) & (v <= 2.0 ** 14), good, 0.0)
    ok_ref[0, 0] = jnp.min(good).astype(jnp.int32)

    cols = m_ref[...].astype(F32).T
    for j in range(m_ref.shape[0]):
        col = jnp.where(jnp.broadcast_to(cols[:, j:j+1], (128, 128)) > 0.0, 0.0, NEG)
        for e in range(8):
            g = 8*j + e
            z, y, x = g // (T*T), (g // T) % T, g % T
            to = (((z+y+x) % T)*2*T*T + (z*T+y)*2) * R
            mask_ref[to:to+2*R] = col[2*R*e:2*R*(e+1)]


def setup(ws, res_mask, R):
    n, C, H = ws[3].shape
    N = res_mask.shape[0]
    ln_w, w_in, b_g, w_b, w_o, b_o = ws
    sds = jax.ShapeDtypeStruct
    out = (sds((n, C, 8), F32), sds((n, 3*C, C), BF16), sds((n, C, 2*C), BF16), sds((n, C, C), BF16), sds((n, H*R, R*C), BF16),
           sds((N, 128), F32), sds((1, 1), jnp.int32))
    vmem, smem = pl.BlockSpec(memory_space=pltpu.VMEM), pl.BlockSpec(memory_space=pltpu.SMEM)
    return pl.pallas_call(functools.partial(setup_kernel, R), in_specs=[vmem]*7, out_specs=[vmem]*6 + [smem], out_shape=out,
                          name="setup")(ln_w, w_in, b_g, jnp.swapaxes(w_b, 1, 2), w_o, b_o, res_mask.reshape(N//128, 128))


def mega_kernel(R, N, C, H, LAG,
                z_ref, mask_ref, cols_ref, wqvt_ref, wk2_ref, wo_ref, wbn_ref,
                out_ref,
                k_s, q_s, v_s, g_s, z_s, o_s, y_s, zt_s, bias_s, x_s, r_s, G,
                a2a_send, a2a_recv, own_sem, ag_send, ag_recv):
    ps, jb = pl.program_id(0), pl.program_id(1)
    n_pass = cols_ref.shape[0]
    me = lax.axis_index('dap')
    n_dev = 2*T*T*T
    others = pl.ds(0, n_dev-1)
    D = C // H
    QB = N // BLOCKS
    KC = 128
    CH = N // KC
    DB = QB // R
    par, nxt = lax.rem(ps, 2), lax.rem(ps + 1, 2)
    q0 = pl.multiple_of(jb * QB, QB)
    core = me % 2
    at = (me // (2*T*T), (me // (2*T)) % T, (me // 2) % T)

    def moved(axis, by):
        p = list(at)
        p[axis] = (p[axis] + by) % T
        return p

    def copy(g, b, k, sel, u0, nu, to, c):
        r = G.at[g, b, sel[0], sel[1], sel[2], core, pl.ds(u0, nu)]
        return pltpu.make_async_remote_copy(r, r, ag_send.at[g, b, k], ag_recv.at[g, b, k],
                                            device_id={'dap': _index(*to, c)}, device_id_type=MESH)

    every = slice(None)
    sizes = ((0, pl.ds(0, 3), every), (pl.ds(0, 2), every, every), (0, every, every), (every,)*3, (0, 0, pl.ds(0, 3)))

    def landed(g, b, k, sem):
        for j in (k, 4) if k == 0 else (k,):
            r = G.at[(g, b) + sizes[j] + (0,)]
            pltpu.make_async_copy(r, r, sem.at[g, b, j]).wait()

    def stage(k, g, b):
        if k > 0:
            landed(g, b, k-1, ag_recv)
        if k == 4:
            for j in range(4):
                landed(g, b, j, ag_send)
            return
        if k == 3:
            r = G.at[g, b, :, :, :, core]
            pltpu.make_async_remote_copy(r, r, ag_send.at[g, b, 3], ag_recv.at[g, b, 3],
                                         device_id={'dap': _index(*at, 1-core)}, device_id_type=MESH).start()
            return
        for (a0, a1, a2), u0, nu in PARTS:
            if k == 0:
                def plane(e, sem):
                    to = list(at)
                    to[a0] = (at[a0] + e % T) % T
                    to[a1] = (at[a1] + e // T) % T
                    copy(g, b, sem, at, u0, nu, to, core).start()
                    return sem
                lax.fori_loop(1, T, plane, 4)
                lax.fori_loop(T, T*T, plane, 0)
                continue
            sel = list(at)
            sel[a0] = every
            for by, half in ((1, 0), (T-1, T//2)):
                if k == 1:
                    sel[a1] = every
                else:
                    sel[a1] = pl.ds(half, T//2)
                    sel[a2] = (at[a2] + T - by) % T
                copy(g, b, k, sel, u0, nu, moved(a2, by), core).start()

    def slot(s, p):
        for k in range(5):
            b = s - k
            if isinstance(s, int):
                if 0 <= b < BLOCKS:
                    stage(k, (p + 1) % 2, b)
                continue
            if k < BLOCKS:
                @pl.when((b >= 0) & (p < n_pass-1))
                def _():
                    stage(k, (p + 1) % 2, b)
            if k > 1:
                @pl.when((b < 0) & (b + 5 < BLOCKS) & (p >= 1))
                def _():
                    stage(k, p % 2, b + 5)

    def put_bias(g, b, rows):
        for h in range(H):
            for t in range(2):
                G[g, b, at[0], at[1], at[2], core, 2*h+t] = rows[h*R:(h+1)*R, t*128:(t+1)*128]

    def col(p, j):
        return cols_ref[p, :, j:j+1]

    def bias_rows(p, y):
        return jnp.dot(wbn_ref[p], y, preferred_element_type=F32).astype(BF16)

    def prep(i):
        y = _ln_t(z_s[i].astype(F32), col(ps, 0), col(ps, 1))
        p = jnp.dot(wqvt_ref[ps], y, preferred_element_type=F32)
        k_s[i] = jnp.dot(y.T, wk2_ref[ps], preferred_element_type=F32).astype(BF16)
        q = p[0:C].astype(BF16).astype(F32) * (LOG2E * D ** -0.5)
        qh = q.astype(BF16)
        ql = (q - qh.astype(F32)).astype(BF16)
        for h in range(H):
            q_s[i, 2*D*h:2*D*h+D] = qh[D*h:D*h+D]
            q_s[i, 2*D*h+D:2*D*h+2*D] = ql[D*h:D*h+D]
        v_s[i] = p[C:2*C].astype(BF16)
        g_s[i] = jax.nn.sigmoid(p[2*C:3*C] + col(ps, 2))

    def prep_all():
        def two(t, _):
            prep(2*t)
            prep(2*t+1)
            return 0
        lax.fori_loop(0, R//2, two, 0)

    def unpack(g, w, by_place):
        src = [16*w + k for k in range(16)]
        if by_place:
            src = [_index(*_place(w // 2, (w % 2)*16 + k)) for k in range(16)]
        t = jnp.concatenate([r_s[g, s] for s in src], axis=0).astype(F32).T
        x = [t[i*C:(i+1)*C] for i in range(R)]
        lane = lax.broadcasted_iota(jnp.int32, (C, 128), 1)
        for bit in (1, 2, 4):
            odd = (lane & bit) != 0
            for i in range(R):
                if not i & bit:
                    a, b = x[i], x[i | bit]
                    x[i] = jnp.where(odd, pltpu.roll(b, bit, 1), a)
                    x[i | bit] = jnp.where(odd, b, pltpu.roll(a, 128-bit, 1))
        for i in range(R):
            z_s[i, :, pl.ds(pl.multiple_of(w*128, 128), 128)] = x[i].astype(BF16)

    def arrived(g, by_place):
        pltpu.make_async_copy(r_s.at[g, others], r_s.at[g, others], a2a_recv.at[g]).wait()
        pltpu.make_async_copy(r_s.at[g, others], r_s.at[g, others], a2a_send).wait()
        def two(t, _):
            unpack(g, 2*t, by_place)
            unpack(g, 2*t+1, by_place)
            return 0
        lax.fori_loop(0, N//256, two, 0)

    @pl.when((jb == 0) & (ps == 0))
    def _():
        barrier = pltpu.get_barrier_semaphore()
        def greet(k, _):
            pl.semaphore_signal(barrier, inc=1, device_id={'dap': (me + k) % n_dev}, device_id_type=MESH)
            return 0
        lax.fori_loop(1, n_dev, greet, 0)
        def first(b, _):
            row = lax.broadcasted_iota(jnp.int32, (N, QB), 0)
            lane = lax.broadcasted_iota(jnp.int32, (N, QB), 1)
            r = lane // R
            z, y = r // (2*T), (r // 2) % T
            x = (b + 2*T - z - y) % T
            turn = (row == (((z*T + y)*T + x)*2 + r % 2)*R + lane % R).astype(F32).astype(BF16)
            qs = pl.ds(pl.multiple_of(b*QB, QB), QB)
            for i in range(R):
                zb = jnp.dot(z_ref[i], turn, preferred_element_type=F32)
                z_s[i, :, qs] = zb.astype(BF16)
                y_s[i*C:(i+1)*C] = _ln_t(zb, col(0, 0), col(0, 1))
            put_bias(0, b, bias_rows(0, y_s[...]))
            return 0
        lax.fori_loop(0, BLOCKS, first, 0)
        pl.semaphore_wait(barrier, n_dev - 1)
        def gather(k):
            def each(b, _):
                stage(k, 0, b)
                return 0
            lax.fori_loop(0, BLOCKS, each, 0)
        gather(0)
        gather(1)
        prep_all()
        gather(2)
        gather(3)
        gather(4)

    @pl.when((jb == 0) & (ps > 0))
    def _():
        arrived(par, True)
        prep_all()
        slot(4, ps-1)

    @pl.when(ps == 0)
    def _():
        def each(h, _):
            for b in range(BLOCKS):
                for t in range(2):
                    v = [G[(0, b) + _place(jb, r) + (2*h+t,)] for r in range(DB)]
                    v = jnp.concatenate(v, axis=0).astype(F32).T * LOG2E
                    rows = slice((2*b+t)*128, (2*b+t+1)*128)
                    for w in range(2):
                        bias_s[h, rows, w*128:(w+1)*128] = v[:, w*128:(w+1)*128] + mask_ref[rows]
            return 0
        lax.fori_loop(0, H, each, 0)

    @pl.when(ps > 0)
    def _():
        def each(h, _):
            for m in range(CH):
                for w in range(2):
                    v = [G[(par, jb) + _place(m // 2, (m % 2)*16 + r) + (2*h+w,)] for r in range(16)]
                    v = jnp.concatenate(v, axis=0).astype(F32)
                    bias_s[h, m*128:(m+1)*128, w*128:(w+1)*128] = v * LOG2E + mask_ref[m*128:(m+1)*128]
            return 0
        lax.fori_loop(0, H, each, 0)

    zl = jnp.zeros((KC, 256-2*C), BF16)
    zp = jnp.zeros((KC, QB), BF16)
    zv = jnp.zeros((D, 256-KC), BF16)
    zq = jnp.zeros((2*D, QB), BF16)
    steps = [(h, c) for h in range(H) for c in range(CH)]
    S = len(steps)
    es, ss, acc, tot = {}, {}, [None]*R, [None]*R
    for n in range(-LAG, S):
        if n >= 0:
            h, c = steps[n]
            b = bias_s[h, c*KC:(c+1)*KC]
            for i in range(R):
                e = jnp.exp2(ss.pop((n, i)) + b)
                es[i] = e.astype(BF16)
                e = jnp.sum(e.reshape(KC//8, 8, QB), axis=0)
                tot[i] = e if c == 0 else tot[i] + e
        for i in range(R):
            rows = []
            w = zp
            if n+LAG < S:
                h2, c2 = steps[n+LAG]
                w = jnp.concatenate([zq]*h2 + [q_s[i, 2*D*h2:2*D*(h2+1), pl.ds(q0, QB)]] + [zq]*(H-1-h2), axis=0)
                rows.append(jnp.concatenate([zl, k_s[i, c2*KC:(c2+1)*KC]], axis=1))
            if n >= 0:
                rows.append(jnp.concatenate([v_s[i, D*h:D*h+D, c*KC:(c+1)*KC], zv], axis=1))
            o = jnp.dot(jnp.concatenate(rows, axis=0), jnp.concatenate([es.pop(i) if n >= 0 else zp, w], axis=0),
                        preferred_element_type=F32)
            if n+LAG < S:
                ss[n+LAG, i] = o[0:KC]
            if n >= 0:
                o = o[-D:]
                acc[i] = o if c == 0 else acc[i] + o
                if c == CH-1:
                    a = acc[i] / jnp.sum(tot[i], axis=0, keepdims=True)
                    o_s[i, D*h:D*h+D] = (g_s[i, D*h:D*h+D, pl.ds(q0, QB)] * a).astype(BF16)

    pn = (ps + 1) % n_pass

    def upd(t, _):
        for j in range(4):
            i = 4*t + j
            u = jnp.dot(wo_ref[ps], o_s[i], preferred_element_type=F32) + col(ps, 3)
            zn = (z_s[i, :, pl.ds(q0, QB)].astype(F32) + u).astype(BF16)
            rows = pl.ds(pl.multiple_of(i*C, C), C)
            zt_s[rows] = zn
            y_s[rows] = _ln_t(zn.astype(F32), col(pn, 0), col(pn, 1))
        return 0
    lax.fori_loop(0, R//4, upd, 0)
    x_s[pl.ds(jb*DB, DB)] = zt_s[...].T.reshape(DB, R, R*C)

    @pl.when(ps < n_pass-1)
    def _():
        put_bias(nxt, jb, bias_rows(pn, y_s[...]))

    def send(k, _):
        d = _index(*_place(jb, k))
        @pl.when(d != me)
        def _():
            pltpu.make_async_remote_copy(x_s.at[jb*DB + k], r_s.at[nxt, me], a2a_send, a2a_recv.at[nxt],
                                         device_id={'dap': d}, device_id_type=MESH).start()
        return 0
    lax.fori_loop(0, DB, send, 0)

    @pl.when((at[0] + at[1] + at[2]) % T == jb)
    def _():
        r_s[nxt, me] = x_s[jb*DB + (at[0]*T + at[1])*2 + core]
    slot(jb, ps)

    @pl.when((ps == n_pass-1) & (jb == BLOCKS-1))
    def _():
        arrived(nxt, False)
        out = pltpu.make_async_copy(z_s, out_ref, own_sem)
        out.start()
        out.wait()


def mega(z, mask, cols, wqvt, wk2, wo, wbn, LAG=2):
    R, C, N = z.shape
    n_pass = cols.shape[0]
    H = wbn.shape[1] // R
    QB = N // BLOCKS
    full = lambda a: pl.BlockSpec(a.shape, lambda p, j: (0,)*a.ndim, pipeline_mode=pl.Buffered(1))
    args = (z, mask, cols, wqvt, wk2, wo, wbn)
    dma = pltpu.SemaphoreType.DMA
    return pl.pallas_call(
        functools.partial(mega_kernel, R, N, C, H, LAG),
        grid=(n_pass, BLOCKS),
        in_specs=[full(a) for a in args],
        out_specs=pl.BlockSpec(memory_space=pl.ANY),
        out_shape=jax.ShapeDtypeStruct((R, C, N), BF16),
        scratch_shapes=[pltpu.VMEM((R, N, 2*C), BF16), pltpu.VMEM((R, 2*C, N), BF16), pltpu.VMEM((R, C, N), BF16),
                        pltpu.VMEM((R, C, N), F32), pltpu.VMEM((R, C, N), BF16), pltpu.VMEM((R, C, QB), BF16),
                        pltpu.VMEM((R*C, QB), BF16), pltpu.VMEM((R*C, QB), BF16), pltpu.VMEM((H, N, QB), F32),
                        pltpu.VMEM((N//R, R, R*C), BF16), pltpu.VMEM((2, N//R, R, R*C), BF16),
                        pltpu.VMEM((2, BLOCKS, T, T, T, 2, 2*H, R, 128), BF16),
                        dma, dma((2,)), dma, dma((2, BLOCKS, 5)), dma((2, BLOCKS, 5))],
        compiler_params=pltpu.CompilerParams(dimension_semantics=("arbitrary", "arbitrary"), vmem_limit_bytes=60*2**20,
                                             collective_id=0, has_side_effects=True),
        cost_estimate=pl.CostEstimate(flops=n_pass*4*R*H*N*N*(C//H), bytes_accessed=4*N*R*C, transcendentals=n_pass*R*H*N*N),
        name="mega",
    )(*args)


def _ln_rows(x, w):
    x = x.astype(F32)
    mu = jnp.mean(x, axis=-1, keepdims=True)
    var = jnp.mean(jnp.square(x - mu), axis=-1, keepdims=True)
    y = (x - mu) * lax.rsqrt(var + EPS)
    return (y * w[0].astype(F32) + w[1].astype(F32)).astype(BF16)


def _rows(zl, bias, lw, wi, bg, wo, bo):
    h, n, _ = bias.shape
    c = zl.shape[-1]
    d = c // h

    def row(zr):
        y = _ln_rows(zr, lw)
        proj = jnp.transpose(jnp.dot(y, wi, preferred_element_type=F32).reshape(n, 4, h, d), (1, 2, 0, 3))
        gate = jax.nn.sigmoid(proj[3] + bg.astype(F32).reshape(h, 1, d))

        def head(a):
            q, k, v, b = a
            s = jnp.dot(q, k.T, preferred_element_type=F32) * d ** -0.5 + b
            return jnp.dot(jax.nn.softmax(s, axis=-1).astype(BF16), v, preferred_element_type=F32)

        o = lax.map(head, (*(a.astype(BF16) for a in proj[:3]), bias))
        o = jnp.transpose((gate * o).astype(BF16), (1, 0, 2)).reshape(n, c)
        return (zr.astype(F32) + jnp.dot(o, wo, preferred_element_type=F32) + bo.astype(F32)).astype(BF16)

    return lax.map(row, zl)


def solution(mesh):
    def local(zl, res_mask, ln_w, w_in, b_g, w_b, w_o, b_o):
        R, N, C = zl.shape
        n = ln_w.shape[0] * ln_w.shape[1]
        ws = tuple(a.reshape(n, *a.shape[2:]) for a in (ln_w, w_in, b_g, w_b, w_o, b_o))
        cols, wqvt, wk2, wo, wbn, mask, ok = setup(ws, res_mask, R)

        def fast(zl):
            return jnp.swapaxes(mega(jnp.swapaxes(zl, 1, 2), mask, cols, wqvt, wk2, wo, wbn), 1, 2)

        def exact(zl):
            mask_bias = jnp.where(res_mask > 0, 0.0, NEG).astype(F32)

            def one(p, z):
                lw, wi, bg, wb, wo, bo = (lax.dynamic_index_in_dim(a, p, keepdims=False) for a in ws)
                b = jnp.dot(_ln_rows(z, lw).reshape(R*N, C), wb, preferred_element_type=F32).astype(BF16)
                b = jnp.transpose(b.reshape(R, 8, N//8, -1), (3, 1, 0, 2))
                b = b.reshape(-1, R, N//8)
                bias = lax.map(lambda a: lax.all_gather(a, 'dap', axis=0, tiled=True), b)
                bias = jnp.swapaxes(bias.reshape(-1, 8, N, N//8), 1, 2).reshape(-1, N, N)
                z = _rows(z, bias.astype(F32) + mask_bias, lw, wi, bg, wo, bo)
                return jnp.swapaxes(lax.all_to_all(z, 'dap', 1, 0, tiled=True), 0, 1)
            return lax.fori_loop(0, n, one, zl)

        return lax.cond(ok[0, 0] > 0, fast, exact, zl)

    rows = P(('data', 'dap'))
    return jax.shard_map(local, mesh=mesh,
                         in_specs=(rows, P('data'), P(), P(), P(), P(), P(), P()),
                         out_specs=rows, check_vma=False)
```

time: 390 us -> 346 us (0.89)
  between operations: 14.2 us -> 0.68 us
  Pallas kernels: 354 us -> 341 us
  local copies, waits for them, and re-layouts: 12.2 us -> 2.37 us
  other arithmetic: 9.04 us -> 0 us
    pallas_call x1 -> x2, Pallas kernels: 354 us -> 341 us  [the longest x1 337 us: mega(): pl.pallas_call(functools.partial(mega_kernel, R, N, C, H, LAG), grid=(n_p...]
    reduce_sum x6 -> x0, other arithmetic: 4.22 us -> none  [the longest x1 2.5 us: _safe_to_skip_max(): gram = jnp.sum(wg[..., :, None] * wg[..., None, :], axis=1)]
where the time goes in v4:
time: 346 us; the launch traced here: 344 us
  Pallas kernels  341 us (99%)
    pallas_call x1, Pallas kernels, mega(): pl.pallas_call(functools.partial(mega_kernel, R, N, C, H, LAG), grid=(n_p...  337 us

profile of v4, /device:TPU:1, one launch (start us, length us, event | category | flops | bytes accessed | tf_op | source)
XLA Modules:
  0.0 344.0 jit_solution(1308402679824361264)
XLA Ops:
  0.0 0.7 reshape.180.bg_ref
  0.7 0.0 copy-start.2
  0.7 0.7 reshape.183.bo_ref
  1.4 0.0 copy-start.3
  1.4 3.9 %setup.1 = (f32[6,64,8]{2,1,0:T(8,128)}, bf16[6,192,64]{2,1,0:T(8,128)(2,1)S(1)}, bf16[6,64,128]{2,1,0:T(8,128)(2,1)}, bf16[6,64,64]{2,1,0:T(8,128)(2,1)}, bf16[...) custom-call(bf16[6,2,64]{2,1,0:T(2,128)(2,1)} %bitcast.230, bf16[6,64,256]{2,1,0:T(8,128)(2,1)} %bitcast.223, ...), custom_call_target="tpu_custom_call" | custom-call | tf_op jit(solution)/shard_map/setup/pallas_call | solution.py:97
  5.9 0.0 copy-done.2
  6.0 0.0 copy-done.3
  6.0 337.0 %conditional.1 = (bf16[8,1024,64]{1,2,0:T(8,128)(2,1)S(1)}) conditional(s32[]{:T(128)} %bitcast.47, (s32[1024]{0:T(1024)}, bf16[6,2,64]{2,1,0:T(2,128)(2,1)}, bf16[6,64,256]{2,1,0:T(8,128)(2,1)}, bf16[6,64]{1,0:T(8,128)(2,1)}, bf16[6,64,4]{1,2,0:T(4,128)(2,1)}, /*index=5*/bf16[6,64,64]{2,1,0:T(8,128)(2,1)}, bf16[6,64]{1,0:T(8,128)(2,1)}, ...), branch_computations={%region_0.15_spmd, %region_15.16_spmd} | conditional | flops 12884901888 | bytes 108475984 | solution.py:467
  6.2 336.8 %mega.1 = bf16[8,64,1024]{2,1,0:T(8,128)(2,1)S(1)} custom-call(bf16[8,64,1024]{2,1,0:T(8,128)(2,1)} %bitcast.222, f32[1024,128]{1,0:T(8,128)} %get-tuple-element.297.mask_ref, f32[6,64,8]{2,1,0:T(8,128)} %get-tuple-element.298.cols_ref, bf16[6,192,64]{2,1,0:T(8,128)(2,1)S(1)} %get-tuple-element.299.wqvt_ref, bf16[6,64,128]{2,1,0:T(8,128)(2,1)} %get-tuple-element.300.wk2_ref, ...), custom_call_target="tpu_custom_call" | custom-call | flops 12884901888 | bytes 2097152 | tf_op jit(solution)/shard_map/cond/branch_1_fun/mega/pallas_call | solution.py:394
  343.0 1.0 copy.110
Async XLA Ops:
  0.7 5.2 %copy-start.2 = (bf16[6,64]{1,0:T(8,128)(2,1)}, bf16[6,64]{1,0:T(8,128)(2,1)S(1)}, u32[]{:S(2)}) copy-start(bf16[6,64]{1,0:T(8,128)(2,1)S(1)} %reshape.180.bg_ref) | copy-start | bytes 2308
  1.4 4.6 %copy-start.3 = (bf16[6,64]{1,0:T(8,128)(2,1)}, bf16[6,64]{1,0:T(8,128)(2,1)S(1)}, u32[]{:S(2)}) copy-start(bf16[6,64]{1,0:T(8,128)(2,1)S(1)} %reshape.183.bo_ref) | copy-start | bytes 2308

commit v5 on v4

--- a/solution.py
+++ b/solution.py
@@ -27,7 +27,11 @@
 
 def _place(b, r):
     z, y = r // (2*T), (r // 2) % T
-    return z, y, (b + 2*T - z - y) % T, r % 2
+    return z, y, 2*(r % 2) + (b // 2 + z + y) % 2, b % 2
+
+
+def _block(z, y, x, c):
+    return (z + y + x) % 2 * 2 + c, (z*T + y)*2 + x // 2
 
 
 def _index(z, y, x, c):
@@ -79,11 +83,10 @@
     cols = m_ref[...].astype(F32).T
     for j in range(m_ref.shape[0]):
         col = jnp.where(jnp.broadcast_to(cols[:, j:j+1], (128, 128)) > 0.0, 0.0, NEG)
-        for e in range(8):
-            g = 8*j + e
-            z, y, x = g // (T*T), (g // T) % T, g % T
-            to = (((z+y+x) % T)*2*T*T + (z*T+y)*2) * R
-            mask_ref[to:to+2*R] = col[2*R*e:2*R*(e+1)]
+        for e in range(16):
+            g = 16*j + e
+            b, r = _block(g // (2*T*T), (g // (2*T)) % T, (g // 2) % T, g % 2)
+            mask_ref[(b*2*T*T + r)*R:(b*2*T*T + r + 1)*R] = col[R*e:R*(e+1)]
 
 
 def setup(ws, res_mask, R):
@@ -117,6 +120,9 @@
     q0 = pl.multiple_of(jb * QB, QB)
     core = me % 2
     at = (me // (2*T*T), (me // (2*T)) % T, (me // 2) % T)
+    my_block, my_place = _block(*at, core)
+    last = ps // (n_pass-1)
+    slot_of_me = (my_block*DB + my_place) * (1-last) + me * last
 
     def moved(axis, by):
         p = list(at)
@@ -151,8 +157,7 @@
         for (a0, a1, a2), u0, nu in PARTS:
             if k == 0:
                 def plane(e, sem):
-                    to = list(at)
-                    to[a0] = (at[a0] + e % T) % T
+                    to = moved(a0, e % T)
                     to[a1] = (at[a1] + e // T) % T
                     copy(g, b, sem, at, u0, nu, to, core).start()
                     return sem
@@ -173,7 +178,7 @@
         for k in range(5):
             b = s - k
             if isinstance(s, int):
-                if 0 <= b < BLOCKS:
+                if 0 < b < BLOCKS:
                     stage(k, (p + 1) % 2, b)
                 continue
             if k < BLOCKS:
@@ -216,11 +221,8 @@
             return 0
         lax.fori_loop(0, R//2, two, 0)
 
-    def unpack(g, w, by_place):
-        src = [16*w + k for k in range(16)]
-        if by_place:
-            src = [_index(*_place(w // 2, (w % 2)*16 + k)) for k in range(16)]
-        t = jnp.concatenate([r_s[g, s] for s in src], axis=0).astype(F32).T
+    def unpack(g, w):
+        t = r_s[g, pl.ds(w*16, 16)].reshape(16*R, R*C).astype(F32).T
         x = [t[i*C:(i+1)*C] for i in range(R)]
         lane = lax.broadcasted_iota(jnp.int32, (C, 128), 1)
         for bit in (1, 2, 4):
@@ -233,14 +235,41 @@
         for i in range(R):
             z_s[i, :, pl.ds(pl.multiple_of(w*128, 128), 128)] = x[i].astype(BF16)
 
-    def arrived(g, by_place):
+    def arrived(g):
         pltpu.make_async_copy(r_s.at[g, others], r_s.at[g, others], a2a_recv.at[g]).wait()
         pltpu.make_async_copy(r_s.at[g, others], r_s.at[g, others], a2a_send).wait()
         def two(t, _):
-            unpack(g, 2*t, by_place)
-            unpack(g, 2*t+1, by_place)
+            unpack(g, 2*t)
+            unpack(g, 2*t+1)
             return 0
         lax.fori_loop(0, N//256, two, 0)
+
+    def to_f32(b, h, m):
+        for w in range(2):
+            v = [G[(par, b) + _place(m // 2, (m % 2)*16 + r) + (2*h+w,)] for r in range(16)]
+            v = jnp.concatenate(v, axis=0).astype(F32)
+            bias_s[h, m*128:(m+1)*128, w*128:(w+1)*128] = v * LOG2E + mask_ref[m*128:(m+1)*128]
+
+    def to_f32_all(b):
+        def each(h, _):
+            for m in range(CH):
+                to_f32(b, h, m)
+            return 0
+        lax.fori_loop(0, H, each, 0)
+
+    def turn_bias(h, _):
+        for b in range(BLOCKS):
+            for a in range(b+1):
+                got = {}
+                for u, v in ((a, b), (b, a))[a == b:]:
+                    for t in range(2):
+                        x = [G[(0, u) + _place(v, r) + (2*h+t,)] for r in range(DB)]
+                        got[u, v, t] = jnp.concatenate(x, axis=0).astype(F32).T.astype(BF16)
+                for (u, v, t), x in got.items():
+                    for r in range(16):
+                        for w in range(2):
+                            G[(0, v) + _place(u, t*16 + r) + (2*h+w,)] = x[r*R:(r+1)*R, w*128:(w+1)*128]
+        return 0
 
     @pl.when((jb == 0) & (ps == 0))
     def _():
@@ -253,9 +282,7 @@
             row = lax.broadcasted_iota(jnp.int32, (N, QB), 0)
             lane = lax.broadcasted_iota(jnp.int32, (N, QB), 1)
             r = lane // R
-            z, y = r // (2*T), (r // 2) % T
-            x = (b + 2*T - z - y) % T
-            turn = (row == (((z*T + y)*T + x)*2 + r % 2)*R + lane % R).astype(F32).astype(BF16)
+            turn = (row == _index(*_place(b, r))*R + lane % R).astype(F32).astype(BF16)
             qs = pl.ds(pl.multiple_of(b*QB, QB), QB)
             for i in range(R):
                 zb = jnp.dot(z_ref[i], turn, preferred_element_type=F32)
@@ -276,36 +303,20 @@
         gather(2)
         gather(3)
         gather(4)
+        lax.fori_loop(0, H, turn_bias, 0)
+        to_f32_all(0)
 
     @pl.when((jb == 0) & (ps > 0))
     def _():
-        arrived(par, True)
+        stage(4, par, 0)
+        to_f32_all(0)
+        arrived(par)
         prep_all()
         slot(4, ps-1)
 
-    @pl.when(ps == 0)
-    def _():
-        def each(h, _):
-            for b in range(BLOCKS):
-                for t in range(2):
-                    v = [G[(0, b) + _place(jb, r) + (2*h+t,)] for r in range(DB)]
-                    v = jnp.concatenate(v, axis=0).astype(F32).T * LOG2E
-                    rows = slice((2*b+t)*128, (2*b+t+1)*128)
-                    for w in range(2):
-                        bias_s[h, rows, w*128:(w+1)*128] = v[:, w*128:(w+1)*128] + mask_ref[rows]
-            return 0
-        lax.fori_loop(0, H, each, 0)
-
-    @pl.when(ps > 0)
-    def _():
-        def each(h, _):
-            for m in range(CH):
-                for w in range(2):
-                    v = [G[(par, jb) + _place(m // 2, (m % 2)*16 + r) + (2*h+w,)] for r in range(16)]
-                    v = jnp.concatenate(v, axis=0).astype(F32)
-                    bias_s[h, m*128:(m+1)*128, w*128:(w+1)*128] = v * LOG2E + mask_ref[m*128:(m+1)*128]
-            return 0
-        lax.fori_loop(0, H, each, 0)
+    @pl.when(jb > 0)
+    def _():
+        to_f32_all(jb)
 
     zl = jnp.zeros((KC, 256-2*C), BF16)
     zp = jnp.zeros((KC, QB), BF16)
@@ -343,41 +354,44 @@
                     a = acc[i] / jnp.sum(tot[i], axis=0, keepdims=True)
                     o_s[i, D*h:D*h+D] = (g_s[i, D*h:D*h+D, pl.ds(q0, QB)] * a).astype(BF16)
 
-    pn = (ps + 1) % n_pass
-
     def upd(t, _):
         for j in range(4):
             i = 4*t + j
             u = jnp.dot(wo_ref[ps], o_s[i], preferred_element_type=F32) + col(ps, 3)
-            zn = (z_s[i, :, pl.ds(q0, QB)].astype(F32) + u).astype(BF16)
-            rows = pl.ds(pl.multiple_of(i*C, C), C)
-            zt_s[rows] = zn
-            y_s[rows] = _ln_t(zn.astype(F32), col(pn, 0), col(pn, 1))
+            zt_s[pl.ds(pl.multiple_of(i*C, C), C)] = (z_s[i, :, pl.ds(q0, QB)].astype(F32) + u).astype(BF16)
         return 0
     lax.fori_loop(0, R//4, upd, 0)
     x_s[pl.ds(jb*DB, DB)] = zt_s[...].T.reshape(DB, R, R*C)
 
+    def send(t, _):
+        for j in range(4):
+            k = 4*t + j
+            d = _index(*_place(jb, k))
+            @pl.when(d != me)
+            def _():
+                pltpu.make_async_remote_copy(x_s.at[jb*DB + k], r_s.at[nxt, slot_of_me], a2a_send, a2a_recv.at[nxt],
+                                             device_id={'dap': d}, device_id_type=MESH).start()
+        return 0
+    lax.fori_loop(0, DB//4, send, 0)
+
+    @pl.when(my_block == jb)
+    def _():
+        r_s[nxt, slot_of_me] = x_s[jb*DB + my_place]
+
     @pl.when(ps < n_pass-1)
     def _():
-        put_bias(nxt, jb, bias_rows(pn, y_s[...]))
-
-    def send(k, _):
-        d = _index(*_place(jb, k))
-        @pl.when(d != me)
-        def _():
-            pltpu.make_async_remote_copy(x_s.at[jb*DB + k], r_s.at[nxt, me], a2a_send, a2a_recv.at[nxt],
-                                         device_id={'dap': d}, device_id_type=MESH).start()
-        return 0
-    lax.fori_loop(0, DB, send, 0)
-
-    @pl.when((at[0] + at[1] + at[2]) % T == jb)
-    def _():
-        r_s[nxt, me] = x_s[jb*DB + (at[0]*T + at[1])*2 + core]
+        def norm(t, _):
+            for j in range(4):
+                rows = pl.ds(pl.multiple_of((4*t + j)*C, C), C)
+                y_s[rows] = _ln_t(zt_s[rows].astype(F32), col(ps+1, 0), col(ps+1, 1))
+            return 0
+        lax.fori_loop(0, R//4, norm, 0)
+        put_bias(nxt, jb, bias_rows(ps+1, y_s[...]))
     slot(jb, ps)
 
     @pl.when((ps == n_pass-1) & (jb == BLOCKS-1))
     def _():
-        arrived(nxt, False)
+        arrived(nxt)
         out = pltpu.make_async_copy(z_s, out_ref, own_sem)
         out.start()
         out.wait()

time: 346 us -> 310 us (0.90)
  Pallas kernels: 341 us -> 303 us
    pallas_call x1, Pallas kernels: 337 us -> 299 us  [mega(): pl.pallas_call(functools.partial(mega_kernel, R, N, C, H, LAG), grid=(n_p...]
where the time goes in v5:
time: 310 us; the launch traced here: 306 us
  Pallas kernels  303 us (98%)
    pallas_call x1, Pallas kernels, mega(): pl.pallas_call(functools.partial(mega_kernel, R, N, C, H, LAG), grid=(n_p...  299 us

profile of v5, /device:TPU:1, one launch (start us, length us, event | category | flops | bytes accessed | tf_op | source)
XLA Modules:
  0.0 305.8 jit_solution(13826222691428833105)
XLA Ops:
  0.0 0.7 reshape.180.bg_ref
  0.7 0.0 copy-start.2
  0.7 0.7 reshape.183.bo_ref
  1.4 0.0 copy-start.3
  1.4 3.9 %setup.1 = (f32[6,64,8]{2,1,0:T(8,128)}, bf16[6,192,64]{2,1,0:T(8,128)(2,1)S(1)}, bf16[6,64,128]{2,1,0:T(8,128)(2,1)}, bf16[6,64,64]{2,1,0:T(8,128)(2,1)}, bf16[...) custom-call(bf16[6,2,64]{2,1,0:T(2,128)(2,1)} %bitcast.230, bf16[6,64,256]{2,1,0:T(8,128)(2,1)} %bitcast.223, ...), custom_call_target="tpu_custom_call" | custom-call | tf_op jit(solution)/shard_map/setup/pallas_call | solution.py:100
  5.9 0.0 copy-done.2
  6.0 0.0 copy-done.3
  6.0 298.9 %conditional.1 = (bf16[8,1024,64]{1,2,0:T(8,128)(2,1)S(1)}) conditional(s32[]{:T(128)} %bitcast.47, (s32[1024]{0:T(1024)}, bf16[6,2,64]{2,1,0:T(2,128)(2,1)}, bf16[6,64,256]{2,1,0:T(8,128)(2,1)}, bf16[6,64]{1,0:T(8,128)(2,1)}, bf16[6,64,4]{1,2,0:T(4,128)(2,1)}, /*index=5*/bf16[6,64,64]{2,1,0:T(8,128)(2,1)}, bf16[6,64]{1,0:T(8,128)(2,1)}, ...), branch_computations={%region_0.15_spmd, %region_15.16_spmd} | conditional | flops 12884901888 | bytes 108475984 | solution.py:481
  6.2 298.6 %mega.1 = bf16[8,64,1024]{2,1,0:T(8,128)(2,1)S(1)} custom-call(bf16[8,64,1024]{2,1,0:T(8,128)(2,1)} %bitcast.222, f32[1024,128]{1,0:T(8,128)} %get-tuple-element.297.mask_ref, f32[6,64,8]{2,1,0:T(8,128)} %get-tuple-element.298.cols_ref, bf16[6,192,64]{2,1,0:T(8,128)(2,1)S(1)} %get-tuple-element.299.wqvt_ref, bf16[6,64,128]{2,1,0:T(8,128)(2,1)} %get-tuple-element.300.wk2_ref, ...), custom_call_target="tpu_custom_call" | custom-call | flops 12884901888 | bytes 2097152 | tf_op jit(solution)/shard_map/cond/branch_1_fun/mega/pallas_call | solution.py:408
  304.8 1.0 copy.110
Async XLA Ops:
  0.7 5.2 %copy-start.2 = (bf16[6,64]{1,0:T(8,128)(2,1)}, bf16[6,64]{1,0:T(8,128)(2,1)S(1)}, u32[]{:S(2)}) copy-start(bf16[6,64]{1,0:T(8,128)(2,1)S(1)} %reshape.180.bg_ref) | copy-start | bytes 2308
  1.4 4.6 %copy-start.3 = (bf16[6,64]{1,0:T(8,128)(2,1)}, bf16[6,64]{1,0:T(8,128)(2,1)S(1)}, u32[]{:S(2)}) copy-start(bf16[6,64]{1,0:T(8,128)(2,1)S(1)} %reshape.183.bo_ref) | copy-start | bytes 2308

commit v6 on v5

--- a/solution.py
+++ b/solution.py
@@ -124,15 +124,18 @@
     last = ps // (n_pass-1)
     slot_of_me = (my_block*DB + my_place) * (1-last) + me * last
 
+    stride = (2*T*T, 2*T, 2)
+    near = [[(at[a] + j) % T for j in range(T)] for a in range(3)]
+    step = [[near[a][j] * stride[a] for j in range(T)] for a in range(3)]
+    home = [step[a][0] for a in range(3)]
+
     def moved(axis, by):
-        p = list(at)
-        p[axis] = (p[axis] + by) % T
-        return p
-
-    def copy(g, b, k, sel, u0, nu, to, c):
+        return core + sum(home[a] for a in range(3) if a != axis) + step[axis][by]
+
+    def copy(g, b, k, sel, u0, nu, to):
         r = G.at[g, b, sel[0], sel[1], sel[2], core, pl.ds(u0, nu)]
         return pltpu.make_async_remote_copy(r, r, ag_send.at[g, b, k], ag_recv.at[g, b, k],
-                                            device_id={'dap': _index(*to, c)}, device_id_type=MESH)
+                                            device_id={'dap': to}, device_id_type=MESH)
 
     every = slice(None)
     sizes = ((0, pl.ds(0, 3), every), (pl.ds(0, 2), every, every), (0, every, every), (every,)*3, (0, 0, pl.ds(0, 3)))
@@ -152,17 +155,18 @@
         if k == 3:
             r = G.at[g, b, :, :, :, core]
             pltpu.make_async_remote_copy(r, r, ag_send.at[g, b, 3], ag_recv.at[g, b, 3],
-                                         device_id={'dap': _index(*at, 1-core)}, device_id_type=MESH).start()
+                                         device_id={'dap': me + 1 - 2*core}, device_id_type=MESH).start()
             return
         for (a0, a1, a2), u0, nu in PARTS:
             if k == 0:
-                def plane(e, sem):
-                    to = moved(a0, e % T)
-                    to[a1] = (at[a1] + e // T) % T
-                    copy(g, b, sem, at, u0, nu, to, core).start()
-                    return sem
-                lax.fori_loop(1, T, plane, 4)
-                lax.fori_loop(T, T*T, plane, 0)
+                for j in range(1, T):
+                    copy(g, b, 4, at, u0, nu, moved(a0, j)).start()
+                def line(f, _):
+                    row = core + home[a2] + (at[a1] + f) % T * stride[a1]
+                    for j in range(T):
+                        copy(g, b, 0, at, u0, nu, row + step[a0][j]).start()
+                    return 0
+                lax.fori_loop(1, T, line, 0)
                 continue
             sel = list(at)
             sel[a0] = every
@@ -171,8 +175,8 @@
                     sel[a1] = every
                 else:
                     sel[a1] = pl.ds(half, T//2)
-                    sel[a2] = (at[a2] + T - by) % T
-                copy(g, b, k, sel, u0, nu, moved(a2, by), core).start()
+                    sel[a2] = near[a2][T-by]
+                copy(g, b, k, sel, u0, nu, moved(a2, by)).start()
 
     def slot(s, p):
         for k in range(5):
@@ -215,11 +219,11 @@
         g_s[i] = jax.nn.sigmoid(p[2*C:3*C] + col(ps, 2))
 
     def prep_all():
-        def two(t, _):
-            prep(2*t)
-            prep(2*t+1)
+        def some(t, _):
+            for j in range(4):
+                prep(4*t+j)
             return 0
-        lax.fori_loop(0, R//2, two, 0)
+        lax.fori_loop(0, R//4, some, 0)
 
     def unpack(g, w):
         t = r_s[g, pl.ds(w*16, 16)].reshape(16*R, R*C).astype(F32).T
@@ -354,13 +358,9 @@
                     a = acc[i] / jnp.sum(tot[i], axis=0, keepdims=True)
                     o_s[i, D*h:D*h+D] = (g_s[i, D*h:D*h+D, pl.ds(q0, QB)] * a).astype(BF16)
 
-    def upd(t, _):
-        for j in range(4):
-            i = 4*t + j
-            u = jnp.dot(wo_ref[ps], o_s[i], preferred_element_type=F32) + col(ps, 3)
-            zt_s[pl.ds(pl.multiple_of(i*C, C), C)] = (z_s[i, :, pl.ds(q0, QB)].astype(F32) + u).astype(BF16)
-        return 0
-    lax.fori_loop(0, R//4, upd, 0)
+    for i in range(R):
+        u = jnp.dot(wo_ref[ps], o_s[i], preferred_element_type=F32) + col(ps, 3)
+        zt_s[i*C:(i+1)*C] = (z_s[i, :, pl.ds(q0, QB)].astype(F32) + u).astype(BF16)
     x_s[pl.ds(jb*DB, DB)] = zt_s[...].T.reshape(DB, R, R*C)
 
     def send(t, _):
@@ -378,15 +378,13 @@
     def _():
         r_s[nxt, slot_of_me] = x_s[jb*DB + my_place]
 
+    pn = (ps + 1) % n_pass
+    for i in range(R):
+        y_s[i*C:(i+1)*C] = _ln_t(zt_s[i*C:(i+1)*C].astype(F32), col(pn, 0), col(pn, 1))
+
     @pl.when(ps < n_pass-1)
     def _():
-        def norm(t, _):
-            for j in range(4):
-                rows = pl.ds(pl.multiple_of((4*t + j)*C, C), C)
-                y_s[rows] = _ln_t(zt_s[rows].astype(F32), col(ps+1, 0), col(ps+1, 1))
-            return 0
-        lax.fori_loop(0, R//4, norm, 0)
-        put_bias(nxt, jb, bias_rows(ps+1, y_s[...]))
+        put_bias(nxt, jb, bias_rows(pn, y_s[...]))
     slot(jb, ps)
 
     @pl.when((ps == n_pass-1) & (jb == BLOCKS-1))

time: 310 us -> 293 us (0.945)
  Pallas kernels: 303 us -> 285 us
    pallas_call x1, Pallas kernels: 299 us -> 281 us  [mega(): pl.pallas_call(functools.partial(mega_kernel, R, N, C, H, LAG), grid=(n_p...]
where the time goes in v6:
time: 293 us; the launch traced here: 289 us
  Pallas kernels  285 us (97%)
    pallas_call x1, Pallas kernels, mega(): pl.pallas_call(functools.partial(mega_kernel, R, N, C, H, LAG), grid=(n_p...  281 us

profile of v6, /device:TPU:1, one launch (start us, length us, event | category | flops | bytes accessed | tf_op | source)
XLA Modules:
  0.0 288.5 jit_solution(536665197948163421)
XLA Ops:
  0.0 0.7 reshape.180.bg_ref
  0.7 0.0 copy-start.2
  0.7 0.7 reshape.183.bo_ref
  1.4 0.0 copy-start.3
  1.4 3.9 %setup.1 = (f32[6,64,8]{2,1,0:T(8,128)}, bf16[6,192,64]{2,1,0:T(8,128)(2,1)S(1)}, bf16[6,64,128]{2,1,0:T(8,128)(2,1)}, bf16[6,64,64]{2,1,0:T(8,128)(2,1)}, bf16[...) custom-call(bf16[6,2,64]{2,1,0:T(2,128)(2,1)} %bitcast.230, bf16[6,64,256]{2,1,0:T(8,128)(2,1)} %bitcast.223, ...), custom_call_target="tpu_custom_call" | custom-call | tf_op jit(solution)/shard_map/setup/pallas_call | solution.py:100
  5.9 0.0 copy-done.2
  6.0 0.0 copy-done.3
  6.0 281.6 %conditional.1 = (bf16[8,1024,64]{1,2,0:T(8,128)(2,1)S(1)}) conditional(s32[]{:T(128)} %bitcast.47, (s32[1024]{0:T(1024)}, bf16[6,2,64]{2,1,0:T(2,128)(2,1)}, bf16[6,64,256]{2,1,0:T(8,128)(2,1)}, bf16[6,64]{1,0:T(8,128)(2,1)}, bf16[6,64,4]{1,2,0:T(4,128)(2,1)}, /*index=5*/bf16[6,64,64]{2,1,0:T(8,128)(2,1)}, bf16[6,64]{1,0:T(8,128)(2,1)}, ...), branch_computations={%region_0.15_spmd, %region_15.16_spmd} | conditional | flops 12884901888 | bytes 108475984 | solution.py:479
  6.2 281.4 %mega.1 = bf16[8,64,1024]{2,1,0:T(8,128)(2,1)S(1)} custom-call(bf16[8,64,1024]{2,1,0:T(8,128)(2,1)} %bitcast.222, f32[1024,128]{1,0:T(8,128)} %get-tuple-element.297.mask_ref, f32[6,64,8]{2,1,0:T(8,128)} %get-tuple-element.298.cols_ref, bf16[6,192,64]{2,1,0:T(8,128)(2,1)S(1)} %get-tuple-element.299.wqvt_ref, bf16[6,64,128]{2,1,0:T(8,128)(2,1)} %get-tuple-element.300.wk2_ref, ...), custom_call_target="tpu_custom_call" | custom-call | flops 12884901888 | bytes 2097152 | tf_op jit(solution)/shard_map/cond/branch_1_fun/mega/pallas_call | solution.py:406
  287.6 1.0 copy.110
Async XLA Ops:
  0.7 5.2 %copy-start.2 = (bf16[6,64]{1,0:T(8,128)(2,1)}, bf16[6,64]{1,0:T(8,128)(2,1)S(1)}, u32[]{:S(2)}) copy-start(bf16[6,64]{1,0:T(8,128)(2,1)S(1)} %reshape.180.bg_ref) | copy-start | bytes 2308
  1.4 4.6 %copy-start.3 = (bf16[6,64]{1,0:T(8,128)(2,1)}, bf16[6,64]{1,0:T(8,128)(2,1)S(1)}, u32[]{:S(2)}) copy-start(bf16[6,64]{1,0:T(8,128)(2,1)S(1)} %reshape.183.bo_ref) | copy-start | bytes 2308

commit v7 on v6

--- a/solution.py
+++ b/solution.py
@@ -179,7 +179,7 @@
                 copy(g, b, k, sel, u0, nu, moved(a2, by)).start()
 
     def slot(s, p):
-        for k in range(5):
+        for k in reversed(range(5)):
             b = s - k
             if isinstance(s, int):
                 if 0 < b < BLOCKS:

time: 293 us -> 300 us (1.024)
  Pallas kernels: 285 us -> 294 us
    pallas_call x1, Pallas kernels: 281 us -> 290 us  [mega(): pl.pallas_call(functools.partial(mega_kernel, R, N, C, H, LAG), grid=(n_p...]
where the time goes in v7:
time: 300 us; the launch traced here: 297 us
  Pallas kernels  294 us (98%)
    pallas_call x1, Pallas kernels, mega(): pl.pallas_call(functools.partial(mega_kernel, R, N, C, H, LAG), grid=(n_p...  290 us

profile of v7, /device:TPU:1, one launch (start us, length us, event | category | flops | bytes accessed | tf_op | source)
XLA Modules:
  0.0 296.9 jit_solution(17909535004479544433)
XLA Ops:
  0.0 0.7 reshape.180.bg_ref
  0.7 0.0 copy-start.2
  0.7 0.7 reshape.183.bo_ref
  1.4 0.0 copy-start.3
  1.4 3.9 %setup.1 = (f32[6,64,8]{2,1,0:T(8,128)}, bf16[6,192,64]{2,1,0:T(8,128)(2,1)S(1)}, bf16[6,64,128]{2,1,0:T(8,128)(2,1)}, bf16[6,64,64]{2,1,0:T(8,128)(2,1)}, bf16[...) custom-call(bf16[6,2,64]{2,1,0:T(2,128)(2,1)} %bitcast.230, bf16[6,64,256]{2,1,0:T(8,128)(2,1)} %bitcast.223, ...), custom_call_target="tpu_custom_call" | custom-call | tf_op jit(solution)/shard_map/setup/pallas_call | solution.py:100
  5.9 0.0 copy-done.2
  6.0 0.0 copy-done.3
  6.0 290.0 %conditional.1 = (bf16[8,1024,64]{1,2,0:T(8,128)(2,1)S(1)}) conditional(s32[]{:T(128)} %bitcast.47, (s32[1024]{0:T(1024)}, bf16[6,2,64]{2,1,0:T(2,128)(2,1)}, bf16[6,64,256]{2,1,0:T(8,128)(2,1)}, bf16[6,64]{1,0:T(8,128)(2,1)}, bf16[6,64,4]{1,2,0:T(4,128)(2,1)}, /*index=5*/bf16[6,64,64]{2,1,0:T(8,128)(2,1)}, bf16[6,64]{1,0:T(8,128)(2,1)}, ...), branch_computations={%region_0.15_spmd, %region_15.16_spmd} | conditional | flops 12884901888 | bytes 108475984 | solution.py:479
  6.2 289.8 %mega.1 = bf16[8,64,1024]{2,1,0:T(8,128)(2,1)S(1)} custom-call(bf16[8,64,1024]{2,1,0:T(8,128)(2,1)} %bitcast.222, f32[1024,128]{1,0:T(8,128)} %get-tuple-element.297.mask_ref, f32[6,64,8]{2,1,0:T(8,128)} %get-tuple-element.298.cols_ref, bf16[6,192,64]{2,1,0:T(8,128)(2,1)S(1)} %get-tuple-element.299.wqvt_ref, bf16[6,64,128]{2,1,0:T(8,128)(2,1)} %get-tuple-element.300.wk2_ref, ...), custom_call_target="tpu_custom_call" | custom-call | flops 12884901888 | bytes 2097152 | tf_op jit(solution)/shard_map/cond/branch_1_fun/mega/pallas_call | solution.py:406
  296.0 1.0 copy.110
Async XLA Ops:
  0.7 5.2 %copy-start.2 = (bf16[6,64]{1,0:T(8,128)(2,1)}, bf16[6,64]{1,0:T(8,128)(2,1)S(1)}, u32[]{:S(2)}) copy-start(bf16[6,64]{1,0:T(8,128)(2,1)S(1)} %reshape.180.bg_ref) | copy-start | bytes 2308
  1.4 4.6 %copy-start.3 = (bf16[6,64]{1,0:T(8,128)(2,1)}, bf16[6,64]{1,0:T(8,128)(2,1)S(1)}, u32[]{:S(2)}) copy-start(bf16[6,64]{1,0:T(8,128)(2,1)S(1)} %reshape.183.bo_ref) | copy-start | bytes 2308
